TPU v7x, 1024 devices: a whole 4x8x16 slice. The times are simulated.
1024 devices in a mesh: ex: 8 (over x, y_lo), ey: 4 (over y_hi), tp: 32 (over z, core).
Axes of the slice: x: 4, y: 8 (y_hi: 4, y_lo: 2; y = y_hi * 2 + y_lo), z: 16, core: 2. Of those that a mesh axis runs over, the one named last changes fastest.
Arguments:
- tokens: bfloat16 [1024, 7168], P(('ex', 'ey'), 'tp'), may hold values from -6 to 6
- cotangent: bfloat16 [1024, 7168], P(('ex', 'ey'), 'tp'), may hold values from -0.59765625 to 0.59765625
- gates: bfloat16 [1024, 8], P(('ex', 'ey')), may hold values from 0.049804688 to 1
- expert_ids: int32 [1024, 8], P(('ex', 'ey')), may hold values from 0 to 31, all different within a row; in each aligned block of 32 rows (0 to 31, 32 to 63, ...) at most 10 rows name the same one
- saved_gate: bfloat16 [1024, 32, 320], P(None, ('ex', 'ey')), may hold values from -6 to 6
- saved_up: bfloat16 [1024, 32, 320], P(None, ('ex', 'ey')), may hold values from -6 to 6
- w_gate: bfloat16 [32, 7168, 1024], P(('ex', 'ey'), 'tp'), may hold values from -0.1875 to 0.1875
- w_up: bfloat16 [32, 7168, 1024], P(('ex', 'ey'), 'tp'), may hold values from -0.1875 to 0.1875
- w_down: bfloat16 [32, 1024, 7168], P(('ex', 'ey'), None, 'tp'), may hold values from -0.375 to 0.375
Outputs:
- grad_tokens: bfloat16 [1024, 7168], P(('ex', 'ey'), 'tp')
- grad_gates: bfloat16 [1024, 8], P(('ex', 'ey'))
- grad_w_gate: bfloat16 [32, 7168, 1024], P(('ex', 'ey'), 'tp')
- grad_w_up: bfloat16 [32, 7168, 1024], P(('ex', 'ey'), 'tp')
- grad_w_down: bfloat16 [32, 1024, 7168], P(('ex', 'ey'), None, 'tp')
Inputs may be any that keep to these rules, and one draw needn't show every extreme that they name: `expert_ids`: each row names 8 different experts. The rows of one token group name any one expert at most 10 times, a bound that some block reaches.
All inputs are finite; a program needn't handle non-finite values.
Results may differ from a plain program's by a relative error of at most 0.025.
Values may be sent and summed in bfloat16 or wider, within the bound.
No kernel may reach another device: no remote copies, remote signals or barrier semaphores. Data moves between devices by JAX's collectives and lax.ppermute only.
A program may use at most 32 MiB of HBM per device.

v0:
```python
import jax
import jax.numpy as jnp
from jax import lax
from jax.sharding import Mesh
from jax.sharding import PartitionSpec as P

EXPERTS = 32
TOP = 8
CAP = 10
TP = ("tp_0", "tp_1")


def in_one_piece(arrays, axis, split_dim, concat_dim, along):
    both = jnp.concatenate(arrays, axis=along)
    whole, at, gathered = (
        lax.all_to_all(both, axis, split_axis=split_dim, concat_axis=concat_dim, tiled=True),
        0,
        [],
    )
    for a in arrays:
        gathered.append(lax.slice_in_dim(whole, at, at + a.shape[along], axis=along))
        at += a.shape[along]
    return tuple(gathered)


def cut_along(array, dim, size):
    dims = array.shape
    blocks = array.reshape(*dims[:dim], size, dims[dim] // size, *dims[dim + 1 :])
    return jnp.moveaxis(blocks, dim, 0)


def summed_on_arrival(array, axis, dim):
    size = lax.axis_size(axis)
    blocks = lax.all_to_all(cut_along(array, dim, size), axis, 0, 0, tiled=True)
    return jnp.sum(blocks.astype(jnp.float32), axis=0)


def in_order(blocks, dim):
    dims = list(blocks.shape[1:])
    dims[dim] *= blocks.shape[0]
    return jnp.moveaxis(blocks, 0, dim).reshape(dims)


def all_blocks(array, axes, order):
    blocks = array[None]
    for k in order:
        blocks = lax.all_gather(blocks, axes[k], axis=0, tiled=True)
    held = [lax.axis_size(axes[k]) for k in reversed(order)]
    blocks = blocks.reshape(*held, *array.shape)
    turned = sorted(range(len(order)), key=lambda place: order[len(order) - 1 - place])
    return blocks.transpose(*turned, *range(len(order), blocks.ndim)).reshape(-1, *array.shape)


def gathered_by_axis(array, axes, order, dim):
    return in_order(all_blocks(array, axes, order), dim)


def slot_codes(expert_ids, capacity, expert_count):
    tok_rows, top_count = expert_ids.shape
    flat = expert_ids.reshape(-1)
    onehot = (flat[:, None] == jnp.arange(expert_count, dtype=jnp.int32)[None, :]).astype(jnp.int32)
    before = jnp.cumsum(onehot, axis=0) - onehot
    position = jnp.sum(before * onehot, axis=1)
    return (flat * capacity + position).reshape(tok_rows, top_count)


def pre_grads(dh_rows, gate_rows, up_rows):
    dh_wide = dh_rows.astype(jnp.float32)
    act_gate = gate_rows.astype(jnp.float32)
    act_up = up_rows.astype(jnp.float32)
    sigm = jax.nn.sigmoid(act_gate)
    d_gate_pre = (dh_wide * act_up * sigm * (1.0 + act_gate * (1.0 - sigm))).astype(jnp.bfloat16)
    d_up_pre = (dh_wide * act_gate * sigm).astype(jnp.bfloat16)
    return (d_gate_pre, d_up_pre)


def on_device(tokens, cotangent, gates, expert_ids, saved_gate, saved_up, w_gate, w_up, w_down):
    expert_count = EXPERTS
    capacity = CAP
    top_count = TOP
    local_width = tokens.shape[1]
    codes = slot_codes(expert_ids, capacity, expert_count)
    slot_rows = jnp.arange(expert_count * capacity, dtype=jnp.int32)
    tables = [
        (codes[:, k][None, :] == slot_rows[:, None]).astype(jnp.bfloat16) for k in range(top_count)
    ]
    chosen = tables[0]
    send_gate = jnp.dot(tables[0], gates[:, 0:1], preferred_element_type=jnp.float32)
    for k in range(1, top_count):
        chosen = chosen + tables[k]
        send_gate = send_gate + jnp.dot(
            tables[k], gates[:, k : k + 1], preferred_element_type=jnp.float32
        )
    send_x = jnp.dot(chosen, tokens, preferred_element_type=jnp.float32).astype(jnp.bfloat16)
    send_dy = jnp.dot(chosen, cotangent, preferred_element_type=jnp.float32).astype(jnp.bfloat16)
    send_x = send_x.reshape(expert_count, capacity, local_width)
    send_dy = send_dy.reshape(expert_count, capacity, local_width)
    send_gate = send_gate.astype(jnp.bfloat16).reshape(expert_count, capacity, 1)
    recv_x, recv_dy, recv_gate = in_one_piece((send_x, send_dy, send_gate), ("ex", "ey"), 0, 1, 2)
    scaled = (recv_gate.astype(jnp.float32) * recv_dy.astype(jnp.float32)).astype(jnp.bfloat16)
    gate_act = saved_gate.astype(jnp.float32)
    hidden = (gate_act * jax.nn.sigmoid(gate_act) * saved_up.astype(jnp.float32)).astype(
        jnp.bfloat16
    )
    out_rows = jnp.einsum("fes,efd->esd", hidden, w_down, preferred_element_type=jnp.float32)
    score_part = jnp.sum(recv_dy.astype(jnp.float32) * out_rows, axis=2).astype(jnp.bfloat16)
    dh_local = summed_on_arrival(
        jnp.einsum("efd,esd->fes", w_down, scaled, preferred_element_type=jnp.float32).astype(
            jnp.bfloat16
        ),
        TP,
        0,
    ).astype(jnp.bfloat16)
    dh_full, score_parts = (
        gathered_by_axis(dh_local, TP, (0, 1), 0),
        gathered_by_axis(score_part[None], TP, (0, 1), 0),
    )
    d_gate_pre, d_up_pre = pre_grads(dh_full, saved_gate, saved_up)
    score = jnp.sum(score_parts.astype(jnp.float32), axis=0).astype(jnp.bfloat16)
    dx_rows = jnp.einsum("fes,edf->esd", d_gate_pre, w_gate, preferred_element_type=jnp.float32)
    dx_rows = dx_rows + jnp.einsum(
        "fes,edf->esd", d_up_pre, w_up, preferred_element_type=jnp.float32
    )
    dx_rows = dx_rows.astype(jnp.bfloat16)
    grad_w_gate = jnp.einsum(
        "esd,fes->edf", recv_x, d_gate_pre, preferred_element_type=jnp.float32
    ).astype(jnp.bfloat16)
    grad_w_up = jnp.einsum(
        "esd,fes->edf", recv_x, d_up_pre, preferred_element_type=jnp.float32
    ).astype(jnp.bfloat16)
    grad_w_down = jnp.einsum(
        "fes,esd->efd", hidden, scaled, preferred_element_type=jnp.float32
    ).astype(jnp.bfloat16)
    score_col = score[:, :, None]
    back_dx, back_score = in_one_piece((dx_rows, score_col), ("ex", "ey"), 1, 0, 2)
    flat_dx = back_dx.reshape(expert_count * capacity, local_width)
    contract = (((0,), (0,)), ((), ()))
    grad_tokens = lax.dot_general(
        chosen, flat_dx, contract, preferred_element_type=jnp.float32
    ).astype(jnp.bfloat16)
    flat_score = back_score.reshape(expert_count * capacity, 1)
    columns = [
        lax.dot_general(tables[k], flat_score, contract, preferred_element_type=jnp.float32)
        for k in range(top_count)
    ]
    grad_gates = jnp.concatenate(columns, axis=1).astype(jnp.bfloat16)
    return (grad_tokens, grad_gates, grad_w_gate, grad_w_up, grad_w_down)


def solution(mesh):
    split = Mesh(
        mesh.devices.reshape(mesh.shape["ex"], mesh.shape["ey"], 16, 2),
        ("ex", "ey", "tp_0", "tp_1"),
    )
    in_specs = (
        P(("ex", "ey"), TP),
        P(("ex", "ey"), TP),
        P(("ex", "ey"), None),
        P(("ex", "ey"), None),
        P(None, ("ex", "ey"), None),
        P(None, ("ex", "ey"), None),
        P(("ex", "ey"), TP, None),
        P(("ex", "ey"), TP, None),
        P(("ex", "ey"), None, TP),
    )
    out_specs = (
        P(("ex", "ey"), TP),
        P(("ex", "ey"), None),
        P(("ex", "ey"), TP, None),
        P(("ex", "ey"), TP, None),
        P(("ex", "ey"), None, TP),
    )
    return jax.shard_map(
        on_device, mesh=split, in_specs=in_specs, out_specs=out_specs, check_vma=False
    )
```

profile of v0, /device:TPU:8, one launch (start us, length us, event | category | flops | bytes accessed | tf_op | source)
XLA Modules:
  0.0 221.1 jit_solution(7481996036598377544)
XLA Ops:
  0.7 0.8 copy.34
  1.7 0.6 reduce-window.6
  2.7 0.3 slice_reduce_fusion.8
  3.0 0.9 convolution_reduce_fusion
  3.9 0.9 convolution_reduce_fusion.1
  4.7 0.9 convolution_reduce_fusion.2
  5.6 0.9 convolution_reduce_fusion.3
  6.4 0.9 convolution_reduce_fusion.4
  7.3 0.9 convolution_reduce_fusion.5
  8.1 0.9 convolution_reduce_fusion.7
  9.0 0.9 convolution_reduce_fusion.6
  9.9 0.2 reshape.280
  10.1 1.0 convolution_convert_fusion.4
  11.2 0.2 convolution_convert_fusion.5
  11.5 0.3 pad_maximum_fusion
  11.8 28.5 %all_to_all.29 = bf16[32,10,449]{2,1,0:T(8,128)(2,1)S(1)} all-to-all(bf16[32,10,449]{2,1,0:T(8,128)(2,1)S(1)} %pad_maximum_fusion), channel_id=1, replica_groups=mesh['ex'=8,'ey'=4,'tp_0'=16,'tp_1'=2] {'ex','ey'}, dimensions={0} | all-to-all | bytes 574720 | tf_op jit(solution)/shard_map/all_to_all | solution.py:16
  40.7 0.4 fusion.10
  41.1 1.2 copy.39
  42.3 17.3 %all-to-all-start.1 = ((bf16[32,32,1,320]{3,1,2,0:T(8,128)(2,1)}), bf16[32,32,1,320]{3,1,2,0:T(8,128)(2,1)S(1)}, u32[]{:S(2)}, u32[]{:S(2)}) async-start(bf16[32,32,1,320]{3,1,2,0:T(8,128)(2,1)} %bitcast.14), calls=%async_computation.1 | async-start | bytes 1572864 | tf_op jit(solution)/shard_map/all_to_all | solution.py:34
  59.6 1.2 copy.44
  60.8 1.2 copy.43
  61.9 1.3 dynamic-slice
  63.9 40.6 %all-to-all-done.1 = bf16[32,32,1,320]{3,1,2,0:T(8,128)(2,1)S(1)} async-done(((bf16[32,32,1,320]{3,1,2,0:T(8,128)(2,1)}), bf16[32,32,1,320]{3,1,2,0:T(8,128)(2,1)S(1)}, u32[]{:S(2)}, u32[]{:S(2)}) %all-to-all-start.1) | async-done | bytes 655392 | tf_op jit(solution)/shard_map/all_to_all | solution.py:34
  104.6 28.4 %all-gather = bf16[512,320]{1,0:T(8,128)(2,1)S(1)} all-gather(bf16[32,320]{1,0:T(8,128)(2,1)S(1)} %reduce_sum.46), channel_id=2, replica_groups=mesh['ex'=8,'ey'=4,'tp_0'=16,'tp_1'=2] {'tp_0'}, dimensions={0}, use_global_device_ids=true | all-gather | bytes 348160 | tf_op jit(solution)/shard_map/all_gather | solution.py:47
  133.0 2.4 %all_gather.13 = bf16[32,32,1,320]{3,1,2,0:T(8,128)(2,1)S(1)} all-gather(bf16[16,32,1,320]{3,1,2,0:T(8,128)(2,1)S(1)} %bitcast.176), channel_id=1, replica_groups=mesh['ex'=8,'ey'=4,'tp_0'=16,'tp_1'=2] {'tp_1'}, dimensions={0}, use_global_device_ids=true | all-gather | bytes 983040 | tf_op jit(solution)/shard_map/all_gather | solution.py:47
  135.7 1.0 copy-done.1
  136.7 0.2 copy-done.2
  137.0 0.9 fusion.9
  137.9 0.5 fusion.16
  138.4 0.3 dynamic-update-slice
  138.7 54.2 %all-reduce = bf16[5120]{0:T(1024)(128)(2,1)S(1)} all-reduce(bf16[5120]{0:T(1024)(128)(2,1)S(1)} %dynamic-update-slice), channel_id=3, replica_groups=mesh['ex'=8,'ey'=4,'tp_0'=16,'tp_1'=2] {'tp_0'}, use_global_device_ids=true, to_apply=%add | all-reduce | flops 5120 | bytes 20480
  193.0 1.8 all_gather.15
  194.9 1.2 fusion.11
  196.2 0.4 fusion.39
  196.6 0.4 fusion.17
  197.1 0.3 copy.51
  197.4 0.5 broadcast.49
  197.9 1.7 reduce.48
  199.6 1.0 reshape.309
  200.5 5.9 %all-to-all-start.2 = ((bf16[32,2,1125]{2,1,0:T(2,128)(2,1)}), bf16[32,2,1125]{2,1,0:T(2,128)(2,1)S(1)}, u32[]{:S(2)}, u32[]{:S(2)}) async-start(bf16[32,2,1125]{2,1,0:T(2,128)(2,1)} %reshape.309), calls=%async_computation.2 | async-start | bytes 294912 | tf_op jit(solution)/shard_map/all_to_all | solution.py:16
  206.4 1.2 fusion.12
  207.6 1.4 fusion.13
  209.0 7.6 %all-to-all-done.2 = bf16[32,2,1125]{2,1,0:T(2,128)(2,1)S(1)} async-done(((bf16[32,2,1125]{2,1,0:T(2,128)(2,1)}), bf16[32,2,1125]{2,1,0:T(2,128)(2,1)S(1)}, u32[]{:S(2)}, u32[]{:S(2)}) %all-to-all-start.2) | async-done | bytes 144032 | tf_op jit(solution)/shard_map/all_to_all | solution.py:16
  216.5 0.3 reshape.310
  216.9 0.9 bitcast_reduce_fusion
  217.9 0.2 slice_reduce_fusion
  219.6 0.9 convolution_convert_fusion.6
  220.5 0.6 concatenate.12
  (47 shorter events, 3.4 us)
Async XLA Ops:
  0.6 40.1 %copy-start = (bf16[1,1024,224]{1,2,0:T(8,128)(2,1)S(1)}, bf16[1,1024,224]{1,2,0:T(8,128)(2,1)}, u32[]{:S(2)}) copy-start(bf16[1,1024,224]{1,2,0:T(8,128)(2,1)} %param.17) | copy-start | bytes 1376260
  0.6 10.5 %copy-start.7 = (bf16[32,224]{1,0:T(8,128)(2,1)S(1)}, bf16[32,224]{1,0:T(8,128)(2,1)}, u32[]{:S(2)}) copy-start(bf16[32,224]{1,0:T(8,128)(2,1)} %param.9) | copy-start | bytes 43012
  41.1 18.5 %copy-start.3 = (bf16[1024,1,320]{0,2,1:T(8,128)(2,1)S(1)}, bf16[1024,1,320]{0,2,1:T(8,128)(2,1)}, u32[]{:S(2)}) copy-start(bf16[1024,1,320]{0,2,1:T(8,128)(2,1)} %param.13) | copy-start | bytes 1966084
  42.3 18.5 %copy-start.4 = (bf16[1024,1,320]{0,2,1:T(8,128)(2,1)S(1)}, bf16[1024,1,320]{0,2,1:T(8,128)(2,1)}, u32[]{:S(2)}) copy-start(bf16[1024,1,320]{0,2,1:T(8,128)(2,1)} %param.14) | copy-start | bytes 1966084
  42.3 62.2 %all-to-all-start.1 = ((bf16[32,32,1,320]{3,1,2,0:T(8,128)(2,1)}), bf16[32,32,1,320]{3,1,2,0:T(8,128)(2,1)S(1)}, u32[]{:S(2)}, u32[]{:S(2)}) async-start(bf16[32,32,1,320]{3,1,2,0:T(8,128)(2,1)} %bitcast.14), calls=%async_computation.1 | async-start | bytes 1572864 | tf_op jit(solution)/shard_map/all_to_all | solution.py:34
  135.6 1.1 copy-start.1
  135.6 1.4 copy-start.2
  194.8 1.4 copy-start.5
  194.8 1.8 copy-start.6
  200.5 16.0 %all-to-all-start.2 = ((bf16[32,2,1125]{2,1,0:T(2,128)(2,1)}), bf16[32,2,1125]{2,1,0:T(2,128)(2,1)S(1)}, u32[]{:S(2)}, u32[]{:S(2)}) async-start(bf16[32,2,1125]{2,1,0:T(2,128)(2,1)} %reshape.309), calls=%async_computation.2 | async-start | bytes 294912 | tf_op jit(solution)/shard_map/all_to_all | solution.py:16
where the time goes:
time: 222 us; the launch traced here: 221 us
  blocking collectives  115 us (52%)
  waiting for transfers between devices  48.2 us (22%)
  starting transfers between devices  23.2 us (10%)
  matrix products  15.7 us (7%)
  local copies, waits for them, and re-layouts  12.9 us (6%)
  other arithmetic  4.27 us (2%)
    unnamed x1, blocking collectives  54.2 us
    all_to_all x1, waiting for transfers between devices, summed_on_arrival(): blocks = lax.all_to_all(cut_along(array, dim, size), axis, 0, 0, tiled=True)  40.6 us
    all_gather x3, blocking collectives, all_blocks(): blocks = lax.all_gather(blocks, axes[k], axis=0, tiled=True)  32.6 us
    all_to_all x1, blocking collectives, in_one_piece(): lax.all_to_all(both, axis, split_axis=split_dim, concat_axis=concat_dim,...  28.5 us
    all_to_all x1, starting transfers between devices, summed_on_arrival(): blocks = lax.all_to_all(cut_along(array, dim, size), axis, 0, 0, tiled=True)  17.3 us
    unnamed x25, local copies, waits for them, and re-layouts  7.74 us
    all_to_all x1, waiting for transfers between devices, in_one_piece(): lax.all_to_all(both, axis, split_axis=split_dim, concat_axis=concat_dim,...  7.58 us
    dot_general x7, matrix products, on_device(): jnp.dot(tables[k], gates[:, k:k + 1], preferred_element_type=jnp.float32)  5.97 us
  transfers between devices with their start and end apart: 2, of which 2 were waited for; matrix products, arithmetic and copies ran while one was open for 3% of the time, Pallas kernels for 0%

commit v1 on v0

v1 whole, which is shorter than its diff:
```python
import jax
import jax.numpy as jnp
from jax import lax
from jax.sharding import Mesh
from jax.sharding import PartitionSpec as P

EXPERTS = 32
CAP = 10
TP = ("tp_0", "tp_1")
EP = ("ex", "ey")
F32 = jnp.float32
BF16 = jnp.bfloat16
ROWS = 16
LANES = 256


def swap_cores(a, chips):
    pairs = [(2 * z + c, 2 * z + 1 - c) for z in range(chips) for c in range(2)]
    return lax.ppermute(a, TP, pairs)


def summed_over_tp(part):
    chips = lax.axis_size("tp_0")
    slots, units = part.shape
    bands = chips // 2
    blocks = part.reshape(bands, slots // bands, 4, units // 4).transpose(2, 0, 1, 3)
    blocks = blocks.reshape(2, 2, bands, slots // bands, units // 4)
    core = lax.axis_index("tp_1")
    kept = lax.dynamic_index_in_dim(blocks, core, 0, False)
    given = lax.dynamic_index_in_dim(blocks, 1 - core, 0, False)
    got = swap_cores(given, chips)
    pair = (kept.astype(F32) + got.astype(F32)).astype(BF16)
    pair = pair.reshape(chips, slots // bands, units // 4)
    terms = lax.all_to_all(pair, "tp_0", 0, 0, tiled=True)
    mine = jnp.sum(terms.astype(F32), axis=0).astype(BF16)
    every = lax.all_gather(mine, TP, axis=0, tiled=False)
    every = every.reshape(2, bands, 2, slots // bands, units // 4)
    return every.transpose(1, 3, 2, 0, 4).reshape(slots, units)


def on_device(tokens, cotangent, gates, expert_ids, saved_gate, saved_up, w_gate, w_up, w_down):
    width = tokens.shape[1]
    rows = tokens.shape[0]
    experts = jnp.arange(EXPERTS, dtype=jnp.int32)
    hits = expert_ids[:, :, None] == experts[None, None, :]
    named = jnp.sum(hits.astype(F32), axis=1)
    gate_of = jnp.sum(jnp.where(hits, gates.astype(F32)[:, :, None], 0.0), axis=1)
    order = jnp.arange(rows, dtype=jnp.int32)
    earlier = (order[:, None] > order[None, :]).astype(BF16)
    place = jnp.dot(earlier, named.astype(BF16), preferred_element_type=F32)
    place = jnp.where(named > 0, place, -1.0).T
    takes = place[:, None, :] == jnp.arange(CAP, dtype=jnp.int32).astype(F32)[None, :, None]
    table = takes.astype(BF16)
    send_x = jnp.einsum("est,td->esd", table, tokens, preferred_element_type=F32).astype(BF16)
    send_dy = jnp.einsum("est,td->esd", table, cotangent, preferred_element_type=F32).astype(BF16)
    send_g = jnp.sum(jnp.where(takes, gate_of.T[:, None, :], 0.0), axis=2, keepdims=True).astype(BF16)
    send_dy = jnp.concatenate([send_dy, send_g], axis=2)
    send_dy = jnp.pad(send_dy, ((0, 0), (0, ROWS - CAP), (0, LANES - width - 1)))
    send_x = jnp.pad(send_x, ((0, 0), (0, ROWS - CAP), (0, LANES - width)))
    recv_dy = lax.all_to_all(send_dy, EP, 0, 0, tiled=True)
    recv_x = lax.all_to_all(send_x, EP, 0, 0, tiled=True)
    recv_dy = recv_dy[:, :CAP].reshape(EXPERTS * CAP, LANES)
    gate = recv_dy[:, width : width + 1].astype(F32)
    dy = recv_dy[:, :width]
    x = recv_x[:, :CAP, :width].reshape(EXPERTS * CAP, width)

    act_gate = saved_gate[:, 0, :].T.astype(F32)
    act_up = saved_up[:, 0, :].T.astype(F32)
    down = w_down[0].T
    part = jnp.dot(dy, down, preferred_element_type=F32).astype(BF16)
    total = summed_over_tp(part).astype(F32)

    scaled = (gate * dy.astype(F32)).astype(BF16)
    sigm = jax.nn.sigmoid(act_gate)
    hidden = (act_gate * sigm * act_up).astype(BF16)
    score = jnp.sum(hidden.astype(F32) * total, axis=1, keepdims=True).astype(BF16)
    dh = gate * total
    d_gate = (dh * act_up * sigm * (1.0 + act_gate * (1.0 - sigm))).astype(BF16)
    d_up = (dh * act_gate * sigm).astype(BF16)
    over_units = (((1,), (1,)), ((), ()))
    dx = lax.dot_general(d_gate, w_gate[0], over_units, preferred_element_type=F32)
    dx = dx + lax.dot_general(d_up, w_up[0], over_units, preferred_element_type=F32)
    back = jnp.concatenate([dx.astype(BF16), score], axis=1).reshape(EXPERTS, CAP, width + 1)
    back = jnp.pad(back, ((0, 0), (0, ROWS - CAP), (0, LANES - width - 1)))
    home = lax.all_to_all(back, EP, 0, 0, tiled=True)

    over_slots = (((0,), (0,)), ((), ()))
    grad_w_gate = lax.dot_general(x, d_gate, over_slots, preferred_element_type=F32).astype(BF16)
    grad_w_up = lax.dot_general(x, d_up, over_slots, preferred_element_type=F32).astype(BF16)
    grad_w_down = lax.dot_general(scaled, hidden, over_slots, preferred_element_type=F32).astype(BF16)

    home = home[:, :CAP].reshape(EXPERTS * CAP, LANES)
    flat = table.reshape(EXPERTS * CAP, rows)
    grad_tokens = lax.dot_general(flat, home[:, :width], over_slots, preferred_element_type=F32).astype(BF16)
    score_home = home[:, width].reshape(EXPERTS, CAP).astype(F32)
    of_pair = jnp.sum(jnp.where(takes, score_home[:, :, None], 0.0), axis=1)
    grad_gates = jnp.sum(jnp.where(hits, of_pair.T[:, None, :], 0.0), axis=2).astype(BF16)
    return (grad_tokens, grad_gates, grad_w_gate[None], grad_w_up[None], grad_w_down.T[None])


def solution(mesh):
    split = Mesh(
        mesh.devices.reshape(mesh.shape["ex"], mesh.shape["ey"], mesh.shape["tp"] // 2, 2),
        ("ex", "ey", "tp_0", "tp_1"),
    )
    in_specs = (
        P(EP, TP),
        P(EP, TP),
        P(EP, None),
        P(EP, None),
        P(None, EP, None),
        P(None, EP, None),
        P(EP, TP, None),
        P(EP, TP, None),
        P(EP, None, TP),
    )
    out_specs = (
        P(EP, TP),
        P(EP, None),
        P(EP, TP, None),
        P(EP, TP, None),
        P(EP, None, TP),
    )
    return jax.shard_map(
        on_device, mesh=split, in_specs=in_specs, out_specs=out_specs, check_vma=False
    )
```

time: 222 us -> 144 us (0.65)
  blocking collectives: 115 us -> 32.6 us
  starting transfers between devices: 23.2 us -> 46.9 us
  matrix products: 15.7 us -> 6.88 us
  waiting for transfers between devices: 48.2 us -> 41 us
  local copies, waits for them, and re-layouts: 12.9 us -> 8.52 us
    unnamed x1 -> x0, blocking collectives: 54.2 us -> none
    all_to_all x1 -> x0, blocking collectives: 28.5 us -> none  [in_one_piece(): lax.all_to_all(both, axis, split_axis=split_dim, concat_axis=concat_dim,...]
    all_to_all x2 -> x4, starting transfers between devices: 23.2 us -> 44.9 us  [the longest x1 16.6 us: on_device(): recv_dy = lax.all_to_all(send_dy, EP, 0, 0, tiled=True)]
    all_to_all x2 -> x4, waiting for transfers between devices: 48.2 us -> 39.4 us  [the longest x1 20.1 us: summed_over_tp(): terms = lax.all_to_all(pair, 'tp_0', 0, 0, tiled=True)]
    dot_general x26 -> x10, matrix products: 15.7 us -> 6.88 us  [the longest x1 1.28 us: on_device(): lax.dot_general(scaled, hidden, over_slots, preferred_element_type=F32)]
    unnamed x25 -> x14, local copies, waits for them, and re-layouts: 7.74 us -> 2.34 us
    reduce_sum x3 -> x6, other arithmetic: 0.25 us -> 3.82 us  [the longest x1 3.04 us: on_device(): jnp.sum(hidden.astype(F32) * total, axis=1, keepdims=True).astype(BF16)]
    all_gather x3 -> x1, blocking collectives: 32.6 us -> 32.6 us  [summed_over_tp(): every = lax.all_gather(mine, TP, axis=0, tiled=False)]
  transfers between devices with their start and end apart: 2 -> 5, of which waited for: 2 -> 4; matrix products, arithmetic and copies ran while one was open for 3% -> 9% of each run, Pallas kernels for 0% -> 0%
where the time goes in v1:
time: 144 us; the launch traced here: 143 us
  starting transfers between devices  46.9 us (33%)
  waiting for transfers between devices  41 us (28%)
  blocking collectives  32.6 us (23%)
  local copies, waits for them, and re-layouts  8.52 us (6%)
  matrix products  6.88 us (5%)
  other arithmetic  6.21 us (4%)
    all_gather x1, blocking collectives, summed_over_tp(): every = lax.all_gather(mine, TP, axis=0, tiled=False)  32.6 us
    all_to_all x1, waiting for transfers between devices, summed_over_tp(): terms = lax.all_to_all(pair, 'tp_0', 0, 0, tiled=True)  20.1 us
    all_to_all x1, starting transfers between devices, on_device(): recv_dy = lax.all_to_all(send_dy, EP, 0, 0, tiled=True)  16.6 us
    all_to_all x1, starting transfers between devices, summed_over_tp(): terms = lax.all_to_all(pair, 'tp_0', 0, 0, tiled=True)  13.7 us
    all_to_all x1, waiting for transfers between devices, on_device(): recv_dy = lax.all_to_all(send_dy, EP, 0, 0, tiled=True)  10.7 us
    all_to_all x1, starting transfers between devices, on_device(): home = lax.all_to_all(back, EP, 0, 0, tiled=True)  9.77 us
    all_to_all x1, waiting for transfers between devices, on_device(): home = lax.all_to_all(back, EP, 0, 0, tiled=True)  8.57 us
    all_to_all x1, starting transfers between devices, on_device(): recv_x = lax.all_to_all(send_x, EP, 0, 0, tiled=True)  4.84 us
  transfers between devices with their start and end apart: 5, of which 4 were waited for; matrix products, arithmetic and copies ran while one was open for 9% of the time, Pallas kernels for 0%

profile of v1, /device:TPU:8, one launch (start us, length us, event | category | flops | bytes accessed | tf_op | source)
XLA Modules:
  0.0 143.0 jit_solution(10931628366960137690)
XLA Ops:
  0.7 0.8 copy.62
  1.5 0.8 copy.65
  2.2 0.2 convert_reduce_fusion.2
  2.5 0.2 convolution_select_fusion
  2.7 0.1 broadcast_compare_fusion
  2.8 0.2 select_reduce_fusion.1
  3.1 0.2 copy.68
  3.3 0.9 convolution_convert_fusion.5
  4.2 0.1 pad_maximum_fusion
  4.3 0.1 copy.77
  4.4 0.8 pad.11.clone
  5.2 16.6 %all-to-all-start = ((bf16[32,16,256]{2,1,0:T(8,128)(2,1)}), bf16[32,16,256]{2,1,0:T(8,128)(2,1)S(1)}, u32[]{:S(2)}, u32[]{:S(2)}) async-start(bf16[32,16,256]{2,1,0:T(8,128)(2,1)} %pad.11.clone), calls=%async_computation | async-start | bytes 524288 | tf_op jit(solution)/shard_map/all_to_all | solution.py:60
  21.8 10.7 %all-to-all-done = bf16[32,16,256]{2,1,0:T(8,128)(2,1)S(1)} async-done(((bf16[32,16,256]{2,1,0:T(8,128)(2,1)}), bf16[32,16,256]{2,1,0:T(8,128)(2,1)S(1)}, u32[]{:S(2)}, u32[]{:S(2)}) %all-to-all-start) | async-done | bytes 262176 | tf_op jit(solution)/shard_map/all_to_all | solution.py:60
  32.6 0.3 convolution_convert_fusion
  32.9 0.5 reshape.85
  33.6 1.9 %collective-permute-start = (bf16[2,8,40,256]{3,2,1,0:T(8,128)(2,1)S(1)}, bf16[2,8,40,256]{3,2,1,0:T(8,128)(2,1)S(1)}, u32[]{:S(2)}, u32[]{:S(2)}) collective-permute-start(bf16[2,8,40,256]{3,2,1,0:T(8,128)(2,1)S(1)} %dynamic-slice_bitcast_fusion), channel_id=1, source_target_pairs={{0,1},{1,0},{2,3},{3,2},{4,5},{5,4},{6,7},{7,6},{8,9},{9,8},{10,11... | collective-permute-start | bytes 983048 | tf_op jit(solution)/shard_map/ppermute | solution.py:19
  35.5 1.6 %collective-permute-done = bf16[2,8,40,256]{3,2,1,0:T(8,128)(2,1)S(1)} collective-permute-done((bf16[2,8,40,256]{3,2,1,0:T(8,128)(2,1)S(1)}, bf16[2,8,40,256]{3,2,1,0:T(8,128)(2,1)S(1)}, u32[]{:S(2)}, u32[]{:S(2)}) %collective-permute-start) | collective-permute-done | bytes 327712 | tf_op jit(solution)/shard_map/ppermute | solution.py:19
  37.1 0.8 fusion.20
  37.9 13.7 %all-to-all-start.1 = ((bf16[16,40,256]{2,1,0:T(8,128)(2,1)}), bf16[16,40,256]{2,1,0:T(8,128)(2,1)S(1)}, u32[]{:S(2)}, u32[]{:S(2)}) async-start(bf16[16,40,256]{2,1,0:T(8,128)(2,1)} %bitcast.9), calls=%async_computation.1 | async-start | bytes 655360 | tf_op jit(solution)/shard_map/all_to_all | solution.py:34
  51.6 0.2 convolution_convert_fusion.4
  51.8 0.1 copy.78
  51.9 0.8 pad.13.clone
  52.7 0.2 convert_reduce_fusion.1
  52.8 20.1 %all-to-all-done.1 = bf16[16,40,256]{2,1,0:T(8,128)(2,1)S(1)} async-done(((bf16[16,40,256]{2,1,0:T(8,128)(2,1)}), bf16[16,40,256]{2,1,0:T(8,128)(2,1)S(1)}, u32[]{:S(2)}, u32[]{:S(2)}) %all-to-all-start.1) | async-done | bytes 327712 | tf_op jit(solution)/shard_map/all_to_all | solution.py:34
  73.0 4.8 %all-to-all-start.3 = ((bf16[32,16,256]{2,1,0:T(8,128)(2,1)}), bf16[32,16,256]{2,1,0:T(8,128)(2,1)S(1)}, u32[]{:S(2)}, u32[]{:S(2)}) async-start(bf16[32,16,256]{2,1,0:T(8,128)(2,1)} %pad.13.clone), calls=%async_computation.3 | async-start | bytes 524288 | tf_op jit(solution)/shard_map/all_to_all | solution.py:61
  77.9 32.6 %all-gather = bf16[1280,256]{1,0:T(8,128)(2,1)S(1)} all-gather(bf16[40,256]{1,0:T(8,128)(2,1)S(1)} %reduce_sum.69), channel_id=2, replica_groups=mesh['ex'=8,'ey'=4,'tp_0'=16,'tp_1'=2] {'tp_0','tp_1'}, dimensions={0}, use_global_device_ids=true | all-gather | bytes 675840 | tf_op jit(solution)/shard_map/all_gather | solution.py:36
  110.5 0.1 convert_bitcast_fusion
  110.6 1.0 copy.71
  111.6 1.0 reshape.92
  112.7 3.0 %multiply_reduce_fusion = (bf16[320]{0:T(512)(128)(2,1)S(1)}, bf16[320,1024]{1,0:T(8,128)(2,1)}, bf16[320,1024]{1,0:T(8,128)(2,1)S(1)}, bf16[320,1024]{1,0:T(8,128)(2,1)S(1)}) fusion(f32[320,1024]{1,0:T(8,128)S(1)} %reshape.92, bf16[1024,1,320]{0,2,1:T(8,128)(2,1)} %param.14, bf16[1024,1,320]{0,2,1:T(8,128)(2,1)} %param.13, f32[320]{0:T(512)S(1)} %convert_reduce_fusion.1), kind=kLoop, calls=%fused_computation.20 | loop fusion | flops 7208640 | bytes 4589440 | tf_op jit(solution)/shard_map/reduce_sum | solution.py:76
  115.8 0.4 fusion.25
  116.1 0.6 copy-done.3
  116.8 0.4 fusion.19
  117.2 0.2 convert_element_type.204
  117.5 0.8 fusion.30
  118.3 9.8 %all-to-all-start.2 = ((bf16[32,16,256]{2,1,0:T(8,128)(2,1)}), bf16[32,16,256]{2,1,0:T(8,128)(2,1)S(1)}, u32[]{:S(2)}, u32[]{:S(2)}) async-start(bf16[32,16,256]{2,1,0:T(8,128)(2,1)} %fusion.30), calls=%async_computation.2 | async-start | bytes 524288 | tf_op jit(solution)/shard_map/all_to_all | solution.py:85
  128.2 0.1 eq.43
  128.3 0.1 reshape.89
  128.4 1.2 fusion.16
  129.6 1.2 fusion.17
  130.8 1.3 fusion.18
  132.1 8.6 %all-to-all-done.2 = bf16[32,16,256]{2,1,0:T(8,128)(2,1)S(1)} async-done(((bf16[32,16,256]{2,1,0:T(8,128)(2,1)}), bf16[32,16,256]{2,1,0:T(8,128)(2,1)S(1)}, u32[]{:S(2)}, u32[]{:S(2)}) %all-to-all-start.2) | async-done | bytes 262176 | tf_op jit(solution)/shard_map/all_to_all | solution.py:85
  140.7 0.2 convert_reduce_fusion
  140.9 0.1 reshape.93
  141.0 0.2 select_reduce_fusion
  141.2 0.2 select_reduce_fusion.2
  141.4 0.7 copy.76
  142.1 0.9 convolution_convert_fusion.6
  (24 shorter events, 0.7 us)
Async XLA Ops:
  0.6 32.0 %copy-start = (bf16[1,1024,224]{1,2,0:T(8,128)(2,1)S(1)}, bf16[1,1024,224]{1,2,0:T(8,128)(2,1)}, u32[]{:S(2)}) copy-start(bf16[1,1024,224]{1,2,0:T(8,128)(2,1)} %param.17) | copy-start | bytes 1376260
  5.2 27.3 %all-to-all-start = ((bf16[32,16,256]{2,1,0:T(8,128)(2,1)}), bf16[32,16,256]{2,1,0:T(8,128)(2,1)S(1)}, u32[]{:S(2)}, u32[]{:S(2)}) async-start(bf16[32,16,256]{2,1,0:T(8,128)(2,1)} %pad.11.clone), calls=%async_computation | async-start | bytes 524288 | tf_op jit(solution)/shard_map/all_to_all | solution.py:60
  33.5 18.1 %copy-start.4 = (bf16[32,224]{1,0:T(8,128)(2,1)S(1)}, bf16[32,224]{1,0:T(8,128)(2,1)}, u32[]{:S(2)}) copy-start(bf16[32,224]{1,0:T(8,128)(2,1)} %param.9) | copy-start | bytes 43012
  33.6 3.5 %collective-permute-start = (bf16[2,8,40,256]{3,2,1,0:T(8,128)(2,1)S(1)}, bf16[2,8,40,256]{3,2,1,0:T(8,128)(2,1)S(1)}, u32[]{:S(2)}, u32[]{:S(2)}) collective-permute-start(bf16[2,8,40,256]{3,2,1,0:T(8,128)(2,1)S(1)} %dynamic-slice_bitcast_fusion), channel_id=1, source_target_pairs={{0,1},{1,0},{2,3},{3,2},{4,5},{5,4},{6,7},{7,6},{8,9},{9,8},{10,11... | collective-permute-start | bytes 983048 | tf_op jit(solution)/shard_map/ppermute | solution.py:19
  37.9 35.1 %all-to-all-start.1 = ((bf16[16,40,256]{2,1,0:T(8,128)(2,1)}), bf16[16,40,256]{2,1,0:T(8,128)(2,1)S(1)}, u32[]{:S(2)}, u32[]{:S(2)}) async-start(bf16[16,40,256]{2,1,0:T(8,128)(2,1)} %bitcast.9), calls=%async_computation.1 | async-start | bytes 655360 | tf_op jit(solution)/shard_map/all_to_all | solution.py:34
  73.0 45.4 %all-to-all-start.3 = ((bf16[32,16,256]{2,1,0:T(8,128)(2,1)}), bf16[32,16,256]{2,1,0:T(8,128)(2,1)S(1)}, u32[]{:S(2)}, u32[]{:S(2)}) async-start(bf16[32,16,256]{2,1,0:T(8,128)(2,1)} %pad.13.clone), calls=%async_computation.3 | async-start | bytes 524288 | tf_op jit(solution)/shard_map/all_to_all | solution.py:61
  112.7 3.1 %copy-start.2 = (bf16[1,224,1024]{2,1,0:T(8,128)(2,1)S(1)}, bf16[1,224,1024]{2,1,0:T(8,128)(2,1)}, u32[]{:S(2)}) copy-start(bf16[1,224,1024]{2,1,0:T(8,128)(2,1)} %param.15) | copy-start | bytes 1376260
  115.8 1.0 copy-start.3
  118.3 22.3 %all-to-all-start.2 = ((bf16[32,16,256]{2,1,0:T(8,128)(2,1)}), bf16[32,16,256]{2,1,0:T(8,128)(2,1)S(1)}, u32[]{:S(2)}, u32[]{:S(2)}) async-start(bf16[32,16,256]{2,1,0:T(8,128)(2,1)} %fusion.30), calls=%async_computation.2 | async-start | bytes 524288 | tf_op jit(solution)/shard_map/all_to_all | solution.py:85
  128.4 2.4 %copy-start.1 = (bf16[320,1024]{1,0:T(8,128)(2,1)S(1)}, bf16[320,1024]{1,0:T(8,128)(2,1)}, u32[]{:S(2)}) copy-start(bf16[320,1024]{1,0:T(8,128)(2,1)} %get-tuple-element.18) | copy-start | bytes 1966084

commit v2 on v1

v2 whole, which is shorter than its diff:
```python
import jax
import jax.numpy as jnp
from jax import lax
from jax.experimental import pallas as pl
from jax.experimental.pallas import tpu as pltpu
from jax.sharding import Mesh
from jax.sharding import PartitionSpec as P

EXPERTS = 32
TOP = 8
CAP = 10
ROWS = 32
WIDTH = 224
UNITS = 1024
SLOTS = 320
PACK = 40
HOME = 16
TP = ("tp_0", "tp_1")
EP = ("ex", "ey")
F32 = jnp.float32
BF16 = jnp.bfloat16
VMEM = pl.BlockSpec(memory_space=pltpu.VMEM)
SMEM = pl.BlockSpec(memory_space=pltpu.SMEM)
OVER_UNITS = (((1,), (1,)), ((), ()))
OVER_ROWS = (((0,), (0,)), ((), ()))


def iota(shape, dim):
    return lax.broadcasted_iota(jnp.int32, shape, dim)


def dot(a, b, dims=(((1,), (0,)), ((), ()))):
    return lax.dot_general(a, b, dims, preferred_element_type=F32)


def places(ids, gates):
    expert = iota((EXPERTS, ROWS), 0)
    named = jnp.zeros((EXPERTS, ROWS), F32)
    weight = jnp.zeros((EXPERTS, ROWS), F32)
    for k in range(TOP):
        hit = ids[k : k + 1, :] == expert
        named = named + jnp.where(hit, 1.0, 0.0)
        if gates is not None:
            weight = weight + jnp.where(hit, gates[k : k + 1, :], 0.0)
    before = jnp.where(iota((ROWS, ROWS), 0) < iota((ROWS, ROWS), 1), 1.0, 0.0).astype(BF16)
    place = dot(named.astype(BF16), before)
    return jnp.where(named > 0.5, place, -1.0), weight


def pack_kernel(ids_ref, gates_ref, tok_ref, cot_ref, out_ref):
    place, weight = places(ids_ref[...], gates_ref[...].astype(F32))
    place = jnp.concatenate([place] * 4, axis=1)
    weight = jnp.concatenate([weight] * 4, axis=1)
    row, lane = iota((PACK, 128), 0), iota((PACK, 128), 1)
    want = row - CAP * (lane // ROWS)
    want = jnp.where((want >= 0) & (want < CAP), want, -2).astype(F32)
    tail = lane >= 3 * ROWS
    tok, cot = tok_ref[...], cot_ref[...]
    zeros = jnp.zeros((ROWS, 64), BF16)
    source = jnp.concatenate(
        [
            tok[:, :128],
            cot[:, :128],
            jnp.concatenate([tok[:, 128:192], cot[:, 128:192]], axis=1),
            jnp.concatenate([tok[:, 192:224], cot[:, 192:224], zeros], axis=1),
        ],
        axis=0,
    )
    at_gate = jnp.where(iota((128, 128), 1) == 64, 1.0, 0.0).astype(BF16)
    for e in range(EXPERTS):
        takes = place[e : e + 1, :] == want
        pick = jnp.where(takes, 1.0, 0.0).astype(BF16)
        gate = jnp.where(takes & tail, weight[e : e + 1, :], 0.0).astype(BF16)
        out_ref[e] = (dot(pick, source) + dot(gate, at_gate)).astype(BF16)


def product_kernel(core_ref, recv_ref, down_ref, kept_ref, given_ref, x_ref, scaled_ref, gate_ref):
    core = core_ref[0]
    to_x = jnp.concatenate([iota((128, 128), 1), iota((128, 128), 1)], axis=0)
    at = iota((256, 128), 0)
    from_x = jnp.where(to_x < 64, to_x, to_x + 64)
    from_x = jnp.where(to_x < 96, from_x, -1)
    from_dy = jnp.where(to_x < 64, to_x + 64, to_x + 96)
    from_dy = jnp.where(to_x < 96, from_dy, -1)
    x_move = jnp.where(at == from_x, 1.0, 0.0).astype(BF16)
    dy_move = jnp.where(at == from_dy, 1.0, 0.0).astype(BF16)
    slot, place = iota((8 * CAP, 8 * PACK), 0), iota((8 * CAP, 8 * PACK), 1)
    base = (slot // CAP) * PACK + slot % CAP
    picks = [jnp.where(place == base + CAP * kind, 1.0, 0.0).astype(BF16) for kind in range(4)]
    dys = []
    for j in range(4):
        got = recv_ref[8 * j : 8 * j + 8].reshape(8 * PACK, 128)
        x_low, dy_low, middle, last = [dot(pick, got) for pick in picks]
        tail = jnp.concatenate([middle, last], axis=1).astype(BF16)
        x_high = dot(tail, x_move)
        dy_high = dot(tail, dy_move)
        x = jnp.concatenate([x_low, x_high[:, :96]], axis=1)
        dy = jnp.concatenate([dy_low, dy_high[:, :96]], axis=1)
        gate = last[:, 64:65]
        rows = slice(8 * CAP * j, 8 * CAP * (j + 1))
        x_ref[rows, :] = x.astype(BF16)
        scaled_ref[rows, :] = (gate * dy).astype(BF16)
        gate_ref[rows, :] = jnp.broadcast_to(gate, (8 * CAP, 128))
        dys.append(dy.astype(BF16))
    dy = jnp.concatenate(dys, axis=0)
    low, high = down_ref[:, :512], down_ref[:, 512:]
    for ref, first in ((given_ref, core == 1), (kept_ref, core == 0)):
        part = dot(dy, jnp.where(first, low, high))
        for v in range(2):
            for b in range(8):
                ref[8 * v + b] = part[40 * b : 40 * b + 40, 256 * v : 256 * v + 256].astype(BF16)


def factors_kernel(gate_ref, up_ref, hidden_ref, by_gate_ref, by_up_ref):
    for b in range(20):
        rows = slice(16 * b, 16 * b + 16)
        gate = gate_ref[rows, :].astype(F32)
        up = up_ref[rows, :].astype(F32)
        sigm = jax.nn.sigmoid(gate)
        by_up = gate * sigm
        hidden_ref[rows, :] = (by_up * up).astype(BF16)
        by_gate_ref[rows, :] = up * sigm * (1.0 + gate * (1.0 - sigm))
        by_up_ref[rows, :] = by_up


def down_kernel(scaled_ref, hidden_ref, wd_ref):
    wd_ref[...] = dot(scaled_ref[...], hidden_ref[...], OVER_ROWS).astype(BF16)


def weights_kernel(x_ref, dg_ref, du_ref, wg_ref, wu_ref):
    wg_ref[...] = dot(x_ref[...], dg_ref[...], OVER_ROWS).astype(BF16)
    wu_ref[...] = dot(x_ref[...], du_ref[...], OVER_ROWS).astype(BF16)


def pair_kernel(kept_ref, got_ref, pair_ref):
    for z in range(kept_ref.shape[0]):
        pair_ref[z] = (kept_ref[z].astype(F32) + got_ref[z].astype(F32)).astype(BF16)


def spread_kernel(terms_ref, copies_ref):
    total = terms_ref[0].astype(F32)
    for z in range(1, terms_ref.shape[0]):
        total = total + terms_ref[z].astype(F32)
    total = total.astype(BF16)
    for z in range(terms_ref.shape[0]):
        copies_ref[z] = total


def grads_kernel(core_ref, own_ref, other_ref, gate_ref, by_gate_ref, by_up_ref, hidden_ref, wg_ref, wu_ref, dg_ref, du_ref, back_ref, dx_ref):
    core = core_ref[0]
    for b in range(8):
        rows = slice(40 * b, 40 * b + 40)
        gate = gate_ref[rows, 0:1]
        score = jnp.zeros((40, 1), F32)
        for c in range(2):
            for v in range(2):
                units = slice(512 * c + 256 * v, 512 * c + 256 * v + 256)
                total = jnp.where(core == c, own_ref[8 * v + b], other_ref[8 * v + b]).astype(F32)
                dh = gate * total
                dg_ref[rows, units] = (dh * by_gate_ref[rows, units]).astype(BF16)
                du_ref[rows, units] = (dh * by_up_ref[rows, units]).astype(BF16)
                score = score + jnp.sum(total * hidden_ref[rows, units].astype(F32), axis=1, keepdims=True)
        dx_ref[rows, :] = jnp.broadcast_to(score, (40, 256))
    dx = dot(dg_ref[...], wg_ref[...], OVER_UNITS) + dot(du_ref[...], wu_ref[...], OVER_UNITS)
    dx_ref[:, :WIDTH] = dx
    out, row = iota((8 * HOME, 8 * CAP), 0), iota((8 * HOME, 8 * CAP), 1)
    spread = (row // CAP == out // HOME) & (row % CAP == out % HOME)
    spread = jnp.where(spread, 1.0, 0.0).astype(BF16)
    for j in range(4):
        block = dx_ref[8 * CAP * j : 8 * CAP * (j + 1), :].astype(BF16)
        back_ref[8 * j : 8 * j + 8] = dot(spread, block).astype(BF16).reshape(8, HOME, 256)


def home_kernel(ids_ref, home_ref, tok_ref, gates_ref):
    ids = ids_ref[...]
    place, _ = places(ids, None)
    slot = iota((HOME, ROWS), 0).astype(F32)
    table = jnp.concatenate([jnp.where(place[e : e + 1, :] == slot, 1.0, 0.0) for e in range(EXPERTS)], axis=0)
    home = home_ref[...].reshape(EXPERTS * HOME, 256)
    tok_ref[...] = dot(table.astype(BF16), home, OVER_ROWS)[:, :WIDTH].astype(BF16)
    score = home[:, WIDTH : WIDTH + 1].astype(F32)
    of_pair = jnp.sum((table * score).reshape(EXPERTS, HOME, ROWS), axis=1)
    expert = iota((EXPERTS, ROWS), 0)
    for k in range(TOP):
        hit = ids[k : k + 1, :] == expert
        gates_ref[k : k + 1, :] = jnp.sum(jnp.where(hit, of_pair, 0.0), axis=0, keepdims=True).astype(BF16)


def near(array):
    return pltpu.with_memory_space_constraint(array, pltpu.VMEM)


def call(body, outs, args, scratch=(), name=None, room=16):
    specs = [SMEM if a.dtype == jnp.int32 and a.ndim == 1 else VMEM for a in args]
    return pl.pallas_call(
        body,
        out_shape=[
            pltpu.VMEM(shape, dtype) if stays else jax.ShapeDtypeStruct(shape, dtype)
            for shape, dtype, stays in outs
        ],
        in_specs=specs,
        out_specs=[VMEM] * len(outs),
        scratch_shapes=list(scratch),
        compiler_params=pltpu.CompilerParams(vmem_limit_bytes=room * 1024 * 1024),
        name=name,
    )(*args)


def on_device(tokens, cotangent, gates, expert_ids, saved_gate, saved_up, w_gate, w_up, w_down):
    ids = expert_ids.T
    core = lax.axis_index("tp_1").reshape(1)
    chips = lax.axis_size("tp_0")
    pairs = [(2 * z + c, 2 * z + 1 - c) for z in range(chips) for c in range(2)]
    send = call(
        pack_kernel, [((EXPERTS, PACK, 128), BF16, False)], [ids, gates.T, tokens, cotangent], name="pack", room=60
    )[0]
    recv = lax.all_to_all(send, EP, 0, 0, tiled=True)
    units = ((SLOTS, UNITS), BF16, True)
    wide = ((SLOTS, UNITS), F32, True)
    hidden, by_gate, by_up = call(
        factors_kernel,
        [units, wide, wide],
        [near(saved_gate[:, 0, :].T), near(saved_up[:, 0, :].T)],
        name="factors",
    )
    recv, hidden, by_gate, by_up = lax.optimization_barrier((recv, hidden, by_gate, by_up))
    half = ((chips, 40, 256), BF16, True)
    kept, given, x, scaled, gate = call(
        product_kernel,
        [half, half, ((SLOTS, WIDTH), BF16, False), ((SLOTS, WIDTH), BF16, True), ((SLOTS, 128), F32, True)],
        [core, near(recv), near(w_down[0].T)],
        name="product",
    )
    weights = ((WIDTH, UNITS), BF16, False)
    got = lax.ppermute(given, TP, pairs)
    grad_w_down = call(down_kernel, [weights], [near(scaled), near(hidden)], name="down")[0]
    got, grad_w_down = lax.optimization_barrier((got, grad_w_down))
    pair = call(pair_kernel, [half], [near(kept), near(got)], name="pair")[0]
    terms = lax.all_to_all(pair, "tp_0", 0, 0, tiled=True)

    copies = call(spread_kernel, [((chips, 40, 256), BF16, False)], [near(terms)], name="spread")[0]
    own = lax.all_to_all(copies, "tp_0", 0, 0, tiled=True)
    other = lax.ppermute(own, TP, pairs)
    d_gate, d_up, back = call(
        grads_kernel,
        [units, units, ((EXPERTS, HOME, 256), BF16, False)],
        [core, near(own), near(other), near(gate), near(by_gate), near(by_up), near(hidden), near(w_gate[0]), near(w_up[0])],
        scratch=[pltpu.VMEM((SLOTS, 256), F32)],
        name="grads",
    )
    home = lax.all_to_all(back, EP, 0, 0, tiled=True)
    grad_w_gate, grad_w_up = call(
        weights_kernel, [weights, weights], [near(x), near(d_gate), near(d_up)], name="weights"
    )
    grad_tokens, grad_gates = call(
        home_kernel, [((ROWS, WIDTH), BF16, False), ((TOP, ROWS), BF16, False)], [ids, near(home)], name="home"
    )
    return (grad_tokens, grad_gates.T, grad_w_gate[None], grad_w_up[None], grad_w_down.T[None])


def solution(mesh):
    split = Mesh(
        mesh.devices.reshape(mesh.shape["ex"], mesh.shape["ey"], mesh.shape["tp"] // 2, 2),
        ("ex", "ey", "tp_0", "tp_1"),
    )
    in_specs = (
        P(EP, TP),
        P(EP, TP),
        P(EP, None),
        P(EP, None),
        P(None, EP, None),
        P(None, EP, None),
        P(EP, TP, None),
        P(EP, TP, None),
        P(EP, None, TP),
    )
    out_specs = (
        P(EP, TP),
        P(EP, None),
        P(EP, TP, None),
        P(EP, TP, None),
        P(EP, None, TP),
    )
    return jax.shard_map(
        on_device, mesh=split, in_specs=in_specs, out_specs=out_specs, check_vma=False
    )
```

time: 144 us -> 124 us (0.86)
  blocking collectives: 32.6 us -> 62.4 us
  starting transfers between devices: 46.9 us -> 25.6 us
  waiting for transfers between devices: 41 us -> 20.3 us
  Pallas kernels: 0 us -> 9.79 us
  matrix products: 6.88 us -> 0 us
  other arithmetic: 6.21 us -> 0 us
  local copies, waits for them, and re-layouts: 8.52 us -> 4.14 us
    all_to_all x0 -> x2, blocking collectives: none -> 62.4 us  [the longest x1 35.8 us: on_device(): terms = lax.all_to_all(pair, 'tp_0', 0, 0, tiled=True)]
    all_gather x1 -> x0, blocking collectives: 32.6 us -> none  [summed_over_tp(): every = lax.all_gather(mine, TP, axis=0, tiled=False)]
    all_to_all x3 -> x1, waiting for transfers between devices: 30.8 us -> 8.48 us  [on_device(): recv = lax.all_to_all(send, EP, 0, 0, tiled=True)]
    all_to_all x3 -> x1, starting transfers between devices: 35.2 us -> 16.6 us  [on_device(): recv = lax.all_to_all(send, EP, 0, 0, tiled=True)]
    pallas_call x0 -> x9, Pallas kernels: none -> 9.79 us  [call(): pl.pallas_call(body, out_shape=[pltpu.VMEM(shape, dtype) if stays else ja...]
    dot_general x10 -> x0, matrix products: 6.88 us -> none  [the longest x1 1.28 us: on_device(): lax.dot_general(scaled, hidden, over_slots, preferred_element_type=F32)]
    all_to_all x1, starting transfers between devices: 9.77 us -> 5.13 us  [on_device(): home = lax.all_to_all(back, EP, 0, 0, tiled=True)]
    reduce_sum x6 -> x0, other arithmetic: 3.82 us -> none  [the longest x1 3.04 us: on_device(): jnp.sum(hidden.astype(F32) * total, axis=1, keepdims=True).astype(BF16)]
  transfers between devices with their start and end apart: 5 -> 4, of which waited for: 4 -> 4; matrix products, arithmetic and copies ran while one was open for 9% -> 0% of each run, Pallas kernels for 0% -> 3%
where the time goes in v2:
time: 124 us; the launch traced here: 123 us
  blocking collectives  62.4 us (50%)
  starting transfers between devices  25.6 us (21%)
  waiting for transfers between devices  20.3 us (16%)
  Pallas kernels  9.79 us (8%)
  local copies, waits for them, and re-layouts  4.14 us (3%)
    all_to_all x1, blocking collectives, on_device(): terms = lax.all_to_all(pair, 'tp_0', 0, 0, tiled=True)  35.8 us
    all_to_all x1, blocking collectives, on_device(): own = lax.all_to_all(copies, 'tp_0', 0, 0, tiled=True)  26.7 us
    all_to_all x1, starting transfers between devices, on_device(): recv = lax.all_to_all(send, EP, 0, 0, tiled=True)  16.6 us
    pallas_call x9, Pallas kernels, call(): pl.pallas_call(body, out_shape=[pltpu.VMEM(shape, dtype) if stays else ja...  9.79 us
    all_to_all x1, waiting for transfers between devices, on_device(): home = lax.all_to_all(back, EP, 0, 0, tiled=True)  9.79 us
    all_to_all x1, waiting for transfers between devices, on_device(): recv = lax.all_to_all(send, EP, 0, 0, tiled=True)  8.48 us
    all_to_all x1, starting transfers between devices, on_device(): home = lax.all_to_all(back, EP, 0, 0, tiled=True)  5.13 us
    unnamed x24, local copies, waits for them, and re-layouts  4.14 us
  transfers between devices with their start and end apart: 4, of which 4 were waited for; matrix products, arithmetic and copies ran while one was open for 0% of the time, Pallas kernels for 3%

profile of v2, /device:TPU:8, one launch (start us, length us, event | category | flops | bytes accessed | tf_op | source)
XLA Modules:
  0.0 123.0 jit_solution(16684747824462214507)
XLA Ops:
  0.6 0.0 copy-start.2
  0.6 2.4 %pack.1 = bf16[32,40,128]{2,1,0:T(8,128)(2,1)} custom-call(s32[8,32]{1,0:T(8,128)} %bitcast.25, bf16[8,32]{1,0:T(8,128)(2,1)} %bitcast.28, bf16[32,224]{1,0:T(8,128)(2,1)} %tok_ref.1, bf16[32,224]{1,0:T(8,128)(2,1)} %cot_ref.1), custom_call_target="tpu_custom_call" | custom-call | tf_op jit(solution)/shard_map/pack/pallas_call | solution.py:195
  3.1 16.6 %all-to-all-start = ((bf16[32,40,128]{2,1,0:T(8,128)(2,1)}), bf16[32,40,128]{2,1,0:T(8,128)(2,1)S(1)}, u32[]{:S(2)}, u32[]{:S(2)}) async-start(bf16[32,40,128]{2,1,0:T(8,128)(2,1)} %pack.1), calls=%async_computation | async-start | bytes 655360 | tf_op jit(solution)/shard_map/all_to_all | solution.py:217
  19.7 0.0 copy-done.2
  19.7 0.0 copy-start.3
  19.7 1.1 copy-done.3
  20.8 0.0 copy-start.6
  20.8 0.6 factors.1
  21.4 0.0 copy-start
  21.4 1.1 copy-done
  22.5 8.5 %all-to-all-done.recv_ref = bf16[32,40,128]{2,1,0:T(8,128)(2,1)S(1)} async-done(((bf16[32,40,128]{2,1,0:T(8,128)(2,1)}), bf16[32,40,128]{2,1,0:T(8,128)(2,1)S(1)}, u32[]{:S(2)}, u32[]{:S(2)}) %all-to-all-start) | async-done | bytes 327712 | tf_op jit(solution)/shard_map/all_to_all | solution.py:217
  30.9 0.0 copy-done.6
  30.9 1.3 %product.1 = (bf16[16,40,256]{2,1,0:T(8,128)(2,1)S(1)}, bf16[16,40,256]{2,1,0:T(8,128)(2,1)S(1)}, bf16[320,224]{1,0:T(8,128)(2,1)S(1)}, bf16[320,224]{1,0:T(8,128)(2,1)S(1)}, f32[320,128]{1,0:T(8,128)S(1)}) custom-call(s32[1]{0:T(128)} %bitcast.1.core_ref, bf16[32,40,128]{2,1,0:T(8,128)(2,1)S(1)} %all-to-all-done.recv_ref, bf16[224,1024]{1,0:T(8,128)(2,1)S(1)} %bitcast.22), custom_call_target="tpu_custom_call" | custom-call | tf_op jit(solution)/shard_map/product/pallas_call | solution.py:195
  32.2 0.0 copy-start.9
  32.3 1.9 %collective-permute-start = (bf16[16,40,256]{2,1,0:T(8,128)(2,1)S(1)}, bf16[16,40,256]{2,1,0:T(8,128)(2,1)S(1)}, u32[]{:S(2)}, u32[]{:S(2)}) collective-permute-start(bf16[16,40,256]{2,1,0:T(8,128)(2,1)S(1)} %get-tuple-element.31), channel_id=1, source_target_pairs={{0,1},{1,0},{2,3},{3,2},{4,5},{5,4},{6,7},{7,6},{8,9},{9,8},{10,11... | collective-permute-start | bytes 983048 | tf_op jit(solution)/shard_map/ppermute | solution.py:235
  34.2 1.2 down.1
  35.4 0.4 collective-permute-done.got_ref
  35.8 0.0 copy-done.9
  35.8 0.0 copy-start.1
  35.8 0.0 copy-start.7
  35.8 0.0 copy-start.8
  35.8 0.1 pair.1
  35.9 35.8 %all_to_all.20.terms_ref = bf16[16,40,256]{2,1,0:T(8,128)(2,1)S(1)} all-to-all(bf16[16,40,256]{2,1,0:T(8,128)(2,1)S(1)} %pair.1), channel_id=1, replica_groups=mesh['ex'=8,'ey'=4,'tp_0'=16,'tp_1'=2] {'tp_0'}, dimensions={0} | all-to-all | bytes 655360 | tf_op jit(solution)/shard_map/all_to_all | solution.py:239
  71.6 0.1 spread.1
  71.7 26.7 %all_to_all.21.own_ref = bf16[16,40,256]{2,1,0:T(8,128)(2,1)S(1)} all-to-all(bf16[16,40,256]{2,1,0:T(8,128)(2,1)S(1)} %spread.1), channel_id=1, replica_groups=mesh['ex'=8,'ey'=4,'tp_0'=16,'tp_1'=2] {'tp_0'}, dimensions={0} | all-to-all | bytes 655360 | tf_op jit(solution)/shard_map/all_to_all | solution.py:242
  98.3 1.9 %collective-permute-start.1 = (bf16[16,40,256]{2,1,0:T(8,128)(2,1)S(1)}, bf16[16,40,256]{2,1,0:T(8,128)(2,1)S(1)}, u32[]{:S(2)}, u32[]{:S(2)}) collective-permute-start(bf16[16,40,256]{2,1,0:T(8,128)(2,1)S(1)} %all_to_all.21.own_ref), channel_id=1, source_target_pairs={{0,1},{1,0},{2,3},{3,2},{4,5},{5,4},{6,7},{7,6},{8,9},{9,8},{10,11... | collective-permute-start | bytes 983048 | tf_op jit(solution)/shard_map/ppermute | solution.py:243
  100.3 1.6 %collective-permute-done.1.other_ref = bf16[16,40,256]{2,1,0:T(8,128)(2,1)S(1)} collective-permute-done((bf16[16,40,256]{2,1,0:T(8,128)(2,1)S(1)}, bf16[16,40,256]{2,1,0:T(8,128)(2,1)S(1)}, u32[]{:S(2)}, u32[]{:S(2)}) %collective-permute-start.1) | collective-permute-done | bytes 327712 | tf_op jit(solution)/shard_map/ppermute | solution.py:243
  101.9 0.0 copy-done.1
  101.9 0.0 copy-done.7
  101.9 0.0 copy-done.8
  101.9 0.0 copy-start.10
  101.9 1.8 %grads.1 = (bf16[320,1024]{1,0:T(8,128)(2,1)S(1)}, bf16[320,1024]{1,0:T(8,128)(2,1)S(1)}, bf16[32,16,256]{2,1,0:T(8,128)(2,1)}) custom-call(s32[1]{0:T(128)} %bitcast.1.core_ref, bf16[16,40,256]{2,1,0:T(8,128)(2,1)S(1)} %all_to_all.21.own_ref, bf16[16,40,256]{2,1,0:T(8,128)(2,1)S(1)} %collective-permute-done.1.other_ref, ...), custom_call_target="tpu_custom_call" | custom-call | tf_op jit(solution)/shard_map/grads/pallas_call | solution.py:195
  103.7 0.0 copy-start.4
  103.7 0.9 copy-done.4
  104.5 0.0 copy-start.11
  104.5 5.1 %all-to-all-start.3 = ((bf16[32,16,256]{2,1,0:T(8,128)(2,1)}), bf16[32,16,256]{2,1,0:T(8,128)(2,1)S(1)}, u32[]{:S(2)}, u32[]{:S(2)}) async-start(bf16[32,16,256]{2,1,0:T(8,128)(2,1)} %get-tuple-element.38), calls=%async_computation.3 | async-start | bytes 524288 | tf_op jit(solution)/shard_map/all_to_all | solution.py:251
  109.7 0.0 copy-done.10
  109.7 0.0 copy-start.5
  109.7 1.1 copy-done.5
  110.8 1.4 %weights.1 = (bf16[224,1024]{1,0:T(8,128)(2,1)}, bf16[224,1024]{1,0:T(8,128)(2,1)}) custom-call(bf16[320,224]{1,0:T(8,128)(2,1)S(1)} %copy-done.10, bf16[320,1024]{1,0:T(8,128)(2,1)S(1)} %get-tuple-element.42.dg_ref, bf16[320,1024]{1,0:T(8,128)(2,1)S(1)} %copy-done.5), custom_call_target="tpu_custom_call" | custom-call | tf_op jit(solution)/shard_map/weights/pallas_call | solution.py:195
  112.2 9.8 %all-to-all-done.3.home_ref = bf16[32,16,256]{2,1,0:T(8,128)(2,1)S(1)} async-done(((bf16[32,16,256]{2,1,0:T(8,128)(2,1)}), bf16[32,16,256]{2,1,0:T(8,128)(2,1)S(1)}, u32[]{:S(2)}, u32[]{:S(2)}) %all-to-all-start.3) | async-done | bytes 262176 | tf_op jit(solution)/shard_map/all_to_all | solution.py:251
  122.0 0.0 copy-done.11
  122.0 1.0 home.1
Async XLA Ops:
  0.6 19.1 %copy-start.2 = (bf16[1024,1,320]{0,2,1:T(8,128)(2,1)S(1)}, bf16[1024,1,320]{0,2,1:T(8,128)(2,1)}, u32[]{:S(2)}) copy-start(bf16[1024,1,320]{0,2,1:T(8,128)(2,1)} %param.13) | copy-start | bytes 1966084
  3.1 27.9 %all-to-all-start = ((bf16[32,40,128]{2,1,0:T(8,128)(2,1)}), bf16[32,40,128]{2,1,0:T(8,128)(2,1)S(1)}, u32[]{:S(2)}, u32[]{:S(2)}) async-start(bf16[32,40,128]{2,1,0:T(8,128)(2,1)} %pack.1), calls=%async_computation | async-start | bytes 655360 | tf_op jit(solution)/shard_map/all_to_all | solution.py:217
  19.7 1.1 copy-start.3
  20.8 10.1 %copy-start.6 = (bf16[1,1024,224]{1,2,0:T(8,128)(2,1)S(1)}, bf16[1,1024,224]{1,2,0:T(8,128)(2,1)}, u32[]{:S(2)}) copy-start(bf16[1,1024,224]{1,2,0:T(8,128)(2,1)} %param.17) | copy-start | bytes 1376260
  21.4 1.1 copy-start
  32.2 3.5 %copy-start.9 = (bf16[320,224]{1,0:T(8,128)(2,1)}, bf16[320,224]{1,0:T(8,128)(2,1)S(1)}, u32[]{:S(2)}) copy-start(bf16[320,224]{1,0:T(8,128)(2,1)S(1)} %get-tuple-element.41.x_ref) | copy-start | bytes 430084
  32.3 3.5 %collective-permute-start = (bf16[16,40,256]{2,1,0:T(8,128)(2,1)S(1)}, bf16[16,40,256]{2,1,0:T(8,128)(2,1)S(1)}, u32[]{:S(2)}, u32[]{:S(2)}) collective-permute-start(bf16[16,40,256]{2,1,0:T(8,128)(2,1)S(1)} %get-tuple-element.31), channel_id=1, source_target_pairs={{0,1},{1,0},{2,3},{3,2},{4,5},{5,4},{6,7},{7,6},{8,9},{9,8},{10,11... | collective-permute-start | bytes 983048 | tf_op jit(solution)/shard_map/ppermute | solution.py:235
  35.8 66.1 %copy-start.1 = (f32[320,1024]{1,0:T(8,128)S(1)}, f32[320,1024]{1,0:T(8,128)}, u32[]{:S(2)}) copy-start(f32[320,1024]{1,0:T(8,128)} %copy-done) | copy-start | bytes 3932164
  35.8 66.1 %copy-start.7 = (bf16[1,224,1024]{2,1,0:T(8,128)(2,1)S(1)}, bf16[1,224,1024]{2,1,0:T(8,128)(2,1)}, u32[]{:S(2)}) copy-start(bf16[1,224,1024]{2,1,0:T(8,128)(2,1)} %param.15) | copy-start | bytes 1376260
  35.8 66.1 %copy-start.8 = (bf16[1,224,1024]{2,1,0:T(8,128)(2,1)S(1)}, bf16[1,224,1024]{2,1,0:T(8,128)(2,1)}, u32[]{:S(2)}) copy-start(bf16[1,224,1024]{2,1,0:T(8,128)(2,1)} %param.16) | copy-start | bytes 1376260
  98.3 3.5 %collective-permute-start.1 = (bf16[16,40,256]{2,1,0:T(8,128)(2,1)S(1)}, bf16[16,40,256]{2,1,0:T(8,128)(2,1)S(1)}, u32[]{:S(2)}, u32[]{:S(2)}) collective-permute-start(bf16[16,40,256]{2,1,0:T(8,128)(2,1)S(1)} %all_to_all.21.own_ref), channel_id=1, source_target_pairs={{0,1},{1,0},{2,3},{3,2},{4,5},{5,4},{6,7},{7,6},{8,9},{9,8},{10,11... | collective-permute-start | bytes 983048 | tf_op jit(solution)/shard_map/ppermute | solution.py:243
  101.9 7.8 %copy-start.10 = (bf16[320,224]{1,0:T(8,128)(2,1)S(1)}, bf16[320,224]{1,0:T(8,128)(2,1)}, u32[]{:S(2)}) copy-start(bf16[320,224]{1,0:T(8,128)(2,1)} %copy-done.9) | copy-start | bytes 430084
  103.7 0.9 copy-start.4
  104.5 17.5 %copy-start.11 = (s32[32,8]{0,1:T(8,128)S(1)}, s32[32,8]{0,1:T(8,128)}, u32[]{:S(2)}) copy-start(s32[32,8]{0,1:T(8,128)} %param.12) | copy-start | bytes 3076
  104.5 17.5 %all-to-all-start.3 = ((bf16[32,16,256]{2,1,0:T(8,128)(2,1)}), bf16[32,16,256]{2,1,0:T(8,128)(2,1)S(1)}, u32[]{:S(2)}, u32[]{:S(2)}) async-start(bf16[32,16,256]{2,1,0:T(8,128)(2,1)} %get-tuple-element.38), calls=%async_computation.3 | async-start | bytes 524288 | tf_op jit(solution)/shard_map/all_to_all | solution.py:251
  109.7 1.1 copy-start.5

commit v3 on v2

--- a/solution.py
+++ b/solution.py
@@ -14,13 +14,15 @@
 UNITS = 1024
 SLOTS = 320
 PACK = 40
-HOME = 16
+HOME = 24
+STAGGER = 9000
 TP = ("tp_0", "tp_1")
 EP = ("ex", "ey")
 F32 = jnp.float32
 BF16 = jnp.bfloat16
 VMEM = pl.BlockSpec(memory_space=pltpu.VMEM)
 SMEM = pl.BlockSpec(memory_space=pltpu.SMEM)
+ANY = pl.BlockSpec(memory_space=pl.ANY)
 OVER_UNITS = (((1,), (1,)), ((), ()))
 OVER_ROWS = (((0,), (0,)), ((), ()))
 
@@ -67,11 +69,16 @@
         axis=0,
     )
     at_gate = jnp.where(iota((128, 128), 1) == 64, 1.0, 0.0).astype(BF16)
+    source = jnp.concatenate([source, at_gate], axis=0)
+    picks = []
     for e in range(EXPERTS):
         takes = place[e : e + 1, :] == want
-        pick = jnp.where(takes, 1.0, 0.0).astype(BF16)
-        gate = jnp.where(takes & tail, weight[e : e + 1, :], 0.0).astype(BF16)
-        out_ref[e] = (dot(pick, source) + dot(gate, at_gate)).astype(BF16)
+        pick = jnp.where(takes, 1.0, 0.0)
+        gate = jnp.where(takes & tail, weight[e : e + 1, :], 0.0)
+        picks.append(jnp.concatenate([pick, gate], axis=1))
+    for j in range(4):
+        part = jnp.concatenate(picks[8 * j : 8 * j + 8], axis=0).astype(BF16)
+        out_ref[8 * j : 8 * j + 8] = dot(part, source).astype(BF16).reshape(8, PACK, 128)
 
 
 def product_kernel(core_ref, recv_ref, down_ref, kept_ref, given_ref, x_ref, scaled_ref, gate_ref):
@@ -119,20 +126,27 @@
         sigm = jax.nn.sigmoid(gate)
         by_up = gate * sigm
         hidden_ref[rows, :] = (by_up * up).astype(BF16)
-        by_gate_ref[rows, :] = up * sigm * (1.0 + gate * (1.0 - sigm))
-        by_up_ref[rows, :] = by_up
+        by_gate_ref[rows, :] = (up * sigm * (1.0 + gate * (1.0 - sigm))).astype(BF16)
+        by_up_ref[rows, :] = by_up.astype(BF16)
 
 
 def down_kernel(scaled_ref, hidden_ref, wd_ref):
     wd_ref[...] = dot(scaled_ref[...], hidden_ref[...], OVER_ROWS).astype(BF16)
 
 
-def weights_kernel(x_ref, dg_ref, du_ref, wg_ref, wu_ref):
-    wg_ref[...] = dot(x_ref[...], dg_ref[...], OVER_ROWS).astype(BF16)
-    wu_ref[...] = dot(x_ref[...], du_ref[...], OVER_ROWS).astype(BF16)
-
-
-def pair_kernel(kept_ref, got_ref, pair_ref):
+def weights_kernel(core_ref, x_ref, own_dg_ref, own_du_ref, dg_ref, du_ref, wg_ref, wu_ref):
+    core = core_ref[0]
+    for half, dg, du in ((core, own_dg_ref, own_du_ref), (1 - core, dg_ref, du_ref)):
+        units = pl.ds(pl.multiple_of(512 * half, 512), 512)
+        wg_ref[:, units] = dot(x_ref[...], dg[...], OVER_ROWS).astype(BF16)
+        wu_ref[:, units] = dot(x_ref[...], du[...], OVER_ROWS).astype(BF16)
+
+
+def pair_kernel(core_ref, kept_ref, got_ref, pair_ref):
+    @pl.when(core_ref[0] == 1)
+    def _():
+        pl.delay(STAGGER)
+
     for z in range(kept_ref.shape[0]):
         pair_ref[z] = (kept_ref[z].astype(F32) + got_ref[z].astype(F32)).astype(BF16)
 
@@ -146,40 +160,65 @@
         copies_ref[z] = total
 
 
-def grads_kernel(core_ref, own_ref, other_ref, gate_ref, by_gate_ref, by_up_ref, hidden_ref, wg_ref, wu_ref, dg_ref, du_ref, back_ref, dx_ref):
-    core = core_ref[0]
+def half_grads(half, half_ref, gate_ref, by_gate_ref, by_up_ref, hidden_ref, wg_ref, wu_ref, dg_out, du_out, dx_ref, dg_ref, du_ref, done, first):
     for b in range(8):
         rows = slice(40 * b, 40 * b + 40)
         gate = gate_ref[rows, 0:1]
         score = jnp.zeros((40, 1), F32)
-        for c in range(2):
-            for v in range(2):
-                units = slice(512 * c + 256 * v, 512 * c + 256 * v + 256)
-                total = jnp.where(core == c, own_ref[8 * v + b], other_ref[8 * v + b]).astype(F32)
-                dh = gate * total
-                dg_ref[rows, units] = (dh * by_gate_ref[rows, units]).astype(BF16)
-                du_ref[rows, units] = (dh * by_up_ref[rows, units]).astype(BF16)
-                score = score + jnp.sum(total * hidden_ref[rows, units].astype(F32), axis=1, keepdims=True)
-        dx_ref[rows, :] = jnp.broadcast_to(score, (40, 256))
-    dx = dot(dg_ref[...], wg_ref[...], OVER_UNITS) + dot(du_ref[...], wu_ref[...], OVER_UNITS)
-    dx_ref[:, :WIDTH] = dx
+        for v in range(2):
+            units = pl.ds(pl.multiple_of(512 * half + 256 * v, 256), 256)
+            here = slice(256 * v, 256 * v + 256)
+            total = half_ref[8 * v + b].astype(F32)
+            dh = gate * total
+            dg_ref[rows, here] = (dh * by_gate_ref[rows, units].astype(F32)).astype(BF16)
+            du_ref[rows, here] = (dh * by_up_ref[rows, units].astype(F32)).astype(BF16)
+            score = score + jnp.sum(total * hidden_ref[rows, units].astype(F32), axis=1, keepdims=True)
+        score = jnp.broadcast_to(score, (40, 256 - WIDTH))
+        dx_ref[rows, WIDTH:] = score if first else dx_ref[rows, WIDTH:] + score
+    copies = [pltpu.make_async_copy(dg_ref, dg_out, done.at[0]), pltpu.make_async_copy(du_ref, du_out, done.at[1])]
+    for copy in copies:
+        copy.start()
+    units = pl.ds(pl.multiple_of(512 * half, 512), 512)
+    dx = dot(dg_ref[...], wg_ref[:, units], OVER_UNITS) + dot(du_ref[...], wu_ref[:, units], OVER_UNITS)
+    dx_ref[:, :WIDTH] = dx if first else dx_ref[:, :WIDTH] + dx
+    return copies
+
+
+def own_kernel(core_ref, *refs):
+    for copy in half_grads(core_ref[0], *refs, True):
+        copy.wait()
+
+
+def other_kernel(core_ref, *refs):
+    shared, own_ref, dg_out, du_out, back_ref, dx_ref, scratch = refs[:7], *refs[7:12], refs[12:]
+    dx_ref[...] = own_ref[...]
+    copies = half_grads(1 - core_ref[0], *shared, dg_out, du_out, dx_ref, *scratch, False)
     out, row = iota((8 * HOME, 8 * CAP), 0), iota((8 * HOME, 8 * CAP), 1)
-    spread = (row // CAP == out // HOME) & (row % CAP == out % HOME)
-    spread = jnp.where(spread, 1.0, 0.0).astype(BF16)
+    block, place = out // HOME, out % HOME
+    same = row // CAP == block
+    low = jnp.where(same & (row % CAP == place), 1.0, 0.0).astype(BF16)
+    high = jnp.where(same & (row % CAP == place - CAP), 1.0, 0.0).astype(BF16)
     for j in range(4):
-        block = dx_ref[8 * CAP * j : 8 * CAP * (j + 1), :].astype(BF16)
-        back_ref[8 * j : 8 * j + 8] = dot(spread, block).astype(BF16).reshape(8, HOME, 256)
+        rows = slice(8 * CAP * j, 8 * CAP * (j + 1))
+        spread = dot(low, dx_ref[rows, :128].astype(BF16)) + dot(high, dx_ref[rows, 128:].astype(BF16))
+        back_ref[8 * j : 8 * j + 8] = spread.astype(BF16).reshape(8, HOME, 128)
+    for copy in copies:
+        copy.wait()
 
 
 def home_kernel(ids_ref, home_ref, tok_ref, gates_ref):
     ids = ids_ref[...]
     place, _ = places(ids, None)
     slot = iota((HOME, ROWS), 0).astype(F32)
-    table = jnp.concatenate([jnp.where(place[e : e + 1, :] == slot, 1.0, 0.0) for e in range(EXPERTS)], axis=0)
-    home = home_ref[...].reshape(EXPERTS * HOME, 256)
-    tok_ref[...] = dot(table.astype(BF16), home, OVER_ROWS)[:, :WIDTH].astype(BF16)
-    score = home[:, WIDTH : WIDTH + 1].astype(F32)
-    of_pair = jnp.sum((table * score).reshape(EXPERTS, HOME, ROWS), axis=1)
+    tables = [jnp.where(place[e : e + 1, :] == slot, 1.0, 0.0) for e in range(EXPERTS)]
+    table = jnp.concatenate(tables, axis=0)
+    past = jnp.where(place >= 0.0, place + CAP, -1.0)
+    later = jnp.concatenate([jnp.where(past[e : e + 1, :] == slot, 1.0, 0.0) for e in range(EXPERTS)], axis=0)
+    home = home_ref[...].reshape(EXPERTS * HOME, 128)
+    tok_ref[:, :128] = dot(table.astype(BF16), home, OVER_ROWS).astype(BF16)
+    tok_ref[:, 128:] = dot(later.astype(BF16), home, OVER_ROWS)[:, : WIDTH - 128].astype(BF16)
+    score = home[:, WIDTH - 128 : WIDTH - 127].astype(F32)
+    of_pair = jnp.sum((later * score).reshape(EXPERTS, HOME, ROWS), axis=1)
     expert = iota((EXPERTS, ROWS), 0)
     for k in range(TOP):
         hit = ids[k : k + 1, :] == expert
@@ -199,7 +238,7 @@
             for shape, dtype, stays in outs
         ],
         in_specs=specs,
-        out_specs=[VMEM] * len(outs),
+        out_specs=[ANY if stays is None else VMEM for _, _, stays in outs],
         scratch_shapes=list(scratch),
         compiler_params=pltpu.CompilerParams(vmem_limit_bytes=room * 1024 * 1024),
         name=name,
@@ -216,10 +255,9 @@
     )[0]
     recv = lax.all_to_all(send, EP, 0, 0, tiled=True)
     units = ((SLOTS, UNITS), BF16, True)
-    wide = ((SLOTS, UNITS), F32, True)
     hidden, by_gate, by_up = call(
         factors_kernel,
-        [units, wide, wide],
+        [units, units, units],
         [near(saved_gate[:, 0, :].T), near(saved_up[:, 0, :].T)],
         name="factors",
     )
@@ -235,22 +273,31 @@
     got = lax.ppermute(given, TP, pairs)
     grad_w_down = call(down_kernel, [weights], [near(scaled), near(hidden)], name="down")[0]
     got, grad_w_down = lax.optimization_barrier((got, grad_w_down))
-    pair = call(pair_kernel, [half], [near(kept), near(got)], name="pair")[0]
+    pair = call(pair_kernel, [half], [core, near(kept), near(got)], name="pair")[0]
     terms = lax.all_to_all(pair, "tp_0", 0, 0, tiled=True)
 
     copies = call(spread_kernel, [((chips, 40, 256), BF16, False)], [near(terms)], name="spread")[0]
     own = lax.all_to_all(copies, "tp_0", 0, 0, tiled=True)
     other = lax.ppermute(own, TP, pairs)
-    d_gate, d_up, back = call(
-        grads_kernel,
-        [units, units, ((EXPERTS, HOME, 256), BF16, False)],
-        [core, near(own), near(other), near(gate), near(by_gate), near(by_up), near(hidden), near(w_gate[0]), near(w_up[0])],
-        scratch=[pltpu.VMEM((SLOTS, 256), F32)],
-        name="grads",
+    wide_half = ((SLOTS, UNITS // 2), BF16, None)
+    drafts = [pltpu.VMEM((SLOTS, UNITS // 2), BF16), pltpu.VMEM((SLOTS, UNITS // 2), BF16), pltpu.SemaphoreType.DMA((2,))]
+    sums = ((SLOTS, 256), F32, True)
+    shared = [near(gate), near(by_gate), near(by_up), near(hidden), near(w_gate[0]), near(w_up[0])]
+    own_dg, own_du, own_dx = call(own_kernel, [wide_half, wide_half, sums], [core, near(own), *shared], drafts, name="own")
+    other, own_dx = lax.optimization_barrier((other, own_dx))
+    dg, du, back = call(
+        other_kernel,
+        [wide_half, wide_half, ((EXPERTS, HOME, 128), BF16, False)],
+        [core, near(other), *shared, near(own_dx)],
+        scratch=[pltpu.VMEM((SLOTS, 256), F32), *drafts],
+        name="other",
     )
     home = lax.all_to_all(back, EP, 0, 0, tiled=True)
     grad_w_gate, grad_w_up = call(
-        weights_kernel, [weights, weights], [near(x), near(d_gate), near(d_up)], name="weights"
+        weights_kernel,
+        [weights, weights],
+        [core, near(x), near(own_dg), near(own_du), near(dg), near(du)],
+        name="weights",
     )
     grad_tokens, grad_gates = call(
         home_kernel, [((ROWS, WIDTH), BF16, False), ((TOP, ROWS), BF16, False)], [ids, near(home)], name="home"

time: 124 us -> 119 us (0.960)
  blocking collectives: 62.4 us -> 49.9 us
  starting transfers between devices: 25.6 us -> 35.4 us
  local copies, waits for them, and re-layouts: 4.14 us -> 1.12 us
    ppermute x1, starting transfers between devices: 1.91 us -> 11.7 us  [on_device(): other = lax.ppermute(own, TP, pairs)]
    all_to_all x1, blocking collectives: 35.8 us -> 28.6 us  [on_device(): terms = lax.all_to_all(pair, 'tp_0', 0, 0, tiled=True)]
    all_to_all x1, blocking collectives: 26.7 us -> 21.4 us  [on_device(): own = lax.all_to_all(copies, 'tp_0', 0, 0, tiled=True)]
    unnamed x24 -> x16, local copies, waits for them, and re-layouts: 4.14 us -> 1.12 us
    ppermute x1, waiting for transfers between devices: 1.59 us -> 0.27 us  [on_device(): other = lax.ppermute(own, TP, pairs)]
    pallas_call x9 -> x10, Pallas kernels: 9.79 us -> 10.9 us  [call(): pl.pallas_call(body, out_shape=[pltpu.VMEM(shape, dtype) if stays else ja...]
  transfers between devices with their start and end apart: 4 -> 4, of which waited for: 4 -> 4; matrix products, arithmetic and copies ran while one was open for 0% -> 0% of each run, Pallas kernels for 3% -> 4%
where the time goes in v3:
time: 119 us; the launch traced here: 118 us
  blocking collectives  49.9 us (42%)
  starting transfers between devices  35.4 us (30%)
  waiting for transfers between devices  19.9 us (17%)
  Pallas kernels  10.9 us (9%)
    all_to_all x1, blocking collectives, on_device(): terms = lax.all_to_all(pair, 'tp_0', 0, 0, tiled=True)  28.6 us
    all_to_all x1, blocking collectives, on_device(): own = lax.all_to_all(copies, 'tp_0', 0, 0, tiled=True)  21.4 us
    all_to_all x1, starting transfers between devices, on_device(): recv = lax.all_to_all(send, EP, 0, 0, tiled=True)  16.6 us
    ppermute x1, starting transfers between devices, on_device(): other = lax.ppermute(own, TP, pairs)  11.7 us
    pallas_call x10, Pallas kernels, call(): pl.pallas_call(body, out_shape=[pltpu.VMEM(shape, dtype) if stays else ja...  10.9 us
    all_to_all x1, waiting for transfers between devices, on_device(): home = lax.all_to_all(back, EP, 0, 0, tiled=True)  9.8 us
    all_to_all x1, waiting for transfers between devices, on_device(): recv = lax.all_to_all(send, EP, 0, 0, tiled=True)  9.46 us
    all_to_all x1, starting transfers between devices, on_device(): home = lax.all_to_all(back, EP, 0, 0, tiled=True)  5.14 us
  transfers between devices with their start and end apart: 4, of which 4 were waited for; matrix products, arithmetic and copies ran while one was open for 0% of the time, Pallas kernels for 4%

profile of v3, /device:TPU:8, one launch (start us, length us, event | category | flops | bytes accessed | tf_op | source)
XLA Modules:
  0.0 118.0 jit_solution(12892804212912719459)
XLA Ops:
  0.6 0.0 copy-start.2
  0.6 2.1 %pack.1 = bf16[32,40,128]{2,1,0:T(8,128)(2,1)} custom-call(s32[8,32]{1,0:T(8,128)} %bitcast.27, bf16[8,32]{1,0:T(8,128)(2,1)} %bitcast.30, bf16[32,224]{1,0:T(8,128)(2,1)} %tok_ref.1, bf16[32,224]{1,0:T(8,128)(2,1)} %cot_ref.1), custom_call_target="tpu_custom_call" | custom-call | tf_op jit(solution)/shard_map/pack/pallas_call | solution.py:234
  2.7 16.6 %all-to-all-start = ((bf16[32,40,128]{2,1,0:T(8,128)(2,1)}), bf16[32,40,128]{2,1,0:T(8,128)(2,1)S(1)}, u32[]{:S(2)}, u32[]{:S(2)}) async-start(bf16[32,40,128]{2,1,0:T(8,128)(2,1)} %pack.1), calls=%async_computation | async-start | bytes 655360 | tf_op jit(solution)/shard_map/all_to_all | solution.py:256
  19.4 0.0 copy-done.2
  19.4 0.0 copy-start.3
  19.4 1.1 copy-done.3
  20.5 0.0 copy-start.4
  20.5 0.7 factors.1
  21.1 9.5 %all-to-all-done.recv_ref = bf16[32,40,128]{2,1,0:T(8,128)(2,1)S(1)} async-done(((bf16[32,40,128]{2,1,0:T(8,128)(2,1)}), bf16[32,40,128]{2,1,0:T(8,128)(2,1)S(1)}, u32[]{:S(2)}, u32[]{:S(2)}) %all-to-all-start) | async-done | bytes 327712 | tf_op jit(solution)/shard_map/all_to_all | solution.py:256
  30.6 0.0 copy-done.4
  30.6 1.3 %product.1 = (bf16[16,40,256]{2,1,0:T(8,128)(2,1)S(1)}, bf16[16,40,256]{2,1,0:T(8,128)(2,1)S(1)}, bf16[320,224]{1,0:T(8,128)(2,1)S(1)}, bf16[320,224]{1,0:T(8,128)(2,1)S(1)}, f32[320,128]{1,0:T(8,128)S(1)}) custom-call(s32[1]{0:T(128)} %bitcast.1.core_ref, bf16[32,40,128]{2,1,0:T(8,128)(2,1)S(1)} %all-to-all-done.recv_ref, bf16[224,1024]{1,0:T(8,128)(2,1)S(1)} %bitcast.26), custom_call_target="tpu_custom_call" | custom-call | tf_op jit(solution)/shard_map/product/pallas_call | solution.py:234
  31.9 0.0 copy-start.5
  31.9 1.9 %collective-permute-start = (bf16[16,40,256]{2,1,0:T(8,128)(2,1)S(1)}, bf16[16,40,256]{2,1,0:T(8,128)(2,1)S(1)}, u32[]{:S(2)}, u32[]{:S(2)}) collective-permute-start(bf16[16,40,256]{2,1,0:T(8,128)(2,1)S(1)} %get-tuple-element.36), channel_id=1, source_target_pairs={{0,1},{1,0},{2,3},{3,2},{4,5},{5,4},{6,7},{7,6},{8,9},{9,8},{10,11... | collective-permute-start | bytes 983048 | tf_op jit(solution)/shard_map/ppermute | solution.py:273
  33.8 1.2 %down.1 = bf16[224,1024]{1,0:T(8,128)(2,1)} custom-call(bf16[320,224]{1,0:T(8,128)(2,1)S(1)} %get-tuple-element.37.scaled_ref, bf16[320,1024]{1,0:T(8,128)(2,1)S(1)} %get-tuple-element.38.hidden_ref.refs_4_), custom_call_target="tpu_custom_call" | custom-call | tf_op jit(solution)/shard_map/down/pallas_call | solution.py:234
  35.0 0.0 copy-done.5
  35.0 0.4 collective-permute-done.got_ref
  35.4 0.1 pair.1
  35.5 28.6 %all_to_all.20.terms_ref = bf16[16,40,256]{2,1,0:T(8,128)(2,1)S(1)} all-to-all(bf16[16,40,256]{2,1,0:T(8,128)(2,1)S(1)} %pair.1), channel_id=1, replica_groups=mesh['ex'=8,'ey'=4,'tp_0'=16,'tp_1'=2] {'tp_0'}, dimensions={0} | all-to-all | bytes 655360 | tf_op jit(solution)/shard_map/all_to_all | solution.py:277
  64.1 0.0 copy-start.1
  64.1 0.1 spread.1
  64.1 0.0 copy-start
  64.2 21.4 %all_to_all.21.refs_0_ = bf16[16,40,256]{2,1,0:T(8,128)(2,1)S(1)} all-to-all(bf16[16,40,256]{2,1,0:T(8,128)(2,1)S(1)} %spread.1), channel_id=1, replica_groups=mesh['ex'=8,'ey'=4,'tp_0'=16,'tp_1'=2] {'tp_0'}, dimensions={0} | all-to-all | bytes 655360 | tf_op jit(solution)/shard_map/all_to_all | solution.py:280
  85.5 11.7 %collective-permute-start.1 = (bf16[16,40,256]{2,1,0:T(8,128)(2,1)S(1)}, bf16[16,40,256]{2,1,0:T(8,128)(2,1)S(1)}, u32[]{:S(2)}, u32[]{:S(2)}) collective-permute-start(bf16[16,40,256]{2,1,0:T(8,128)(2,1)S(1)} %all_to_all.21.refs_0_), channel_id=1, source_target_pairs={{0,1},{1,0},{2,3},{3,2},{4,5},{5,4},{6,7},{7,6},{8,9},{9,8},{10,11... | collective-permute-start | bytes 983048 | tf_op jit(solution)/shard_map/ppermute | solution.py:281
  97.2 0.0 copy-done.1
  97.3 0.0 copy-done
  97.3 0.9 own.1
  98.2 0.3 collective-permute-done.1.refs_0_
  98.5 2.1 %other.1 = (bf16[320,512]{1,0:T(8,128)(2,1)S(1)}, bf16[320,512]{1,0:T(8,128)(2,1)S(1)}, bf16[32,24,128]{2,1,0:T(8,128)(2,1)}) custom-call(s32[1]{0:T(128)} %bitcast.1.core_ref, bf16[16,40,256]{2,1,0:T(8,128)(2,1)S(1)} %collective-permute-done.1.refs_0_, f32[320,128]{1,0:T(8,128)S(1)} %get-tuple-element.40.refs_1_, ...), custom_call_target="tpu_custom_call" | custom-call | tf_op jit(solution)/shard_map/other/pallas_call | solution.py:234
  100.6 0.0 copy-start.6
  100.6 5.1 %all-to-all-start.3 = ((bf16[32,24,128]{2,1,0:T(8,128)(2,1)}), bf16[32,24,128]{2,1,0:T(8,128)(2,1)S(1)}, u32[]{:S(2)}, u32[]{:S(2)}) async-start(bf16[32,24,128]{2,1,0:T(8,128)(2,1)} %get-tuple-element.46), calls=%async_computation.3 | async-start | bytes 393216 | tf_op jit(solution)/shard_map/all_to_all | solution.py:295
  105.7 0.0 copy-done.6
  105.7 0.0 copy-start.7
  105.7 1.5 %weights.1 = (bf16[224,1024]{1,0:T(8,128)(2,1)}, bf16[224,1024]{1,0:T(8,128)(2,1)}) custom-call(s32[1]{0:T(128)} %bitcast.1.core_ref, bf16[320,224]{1,0:T(8,128)(2,1)S(1)} %copy-done.6, bf16[320,512]{1,0:T(8,128)(2,1)S(1)} %get-tuple-element.50.own_dg_ref, bf16[320,512]{1,0:T(8,128)(2,1)S(1)} %get-tuple-element.51.own_du_ref, ...), custom_call_target="tpu_custom_call" | custom-call | tf_op jit(solution)/shard_map/weights/pallas_call | solution.py:234
  107.2 9.8 %all-to-all-done.3.home_ref = bf16[32,24,128]{2,1,0:T(8,128)(2,1)S(1)} async-done(((bf16[32,24,128]{2,1,0:T(8,128)(2,1)}), bf16[32,24,128]{2,1,0:T(8,128)(2,1)S(1)}, u32[]{:S(2)}, u32[]{:S(2)}) %all-to-all-start.3) | async-done | bytes 196640 | tf_op jit(solution)/shard_map/all_to_all | solution.py:295
  117.0 0.0 copy-done.7
  117.0 1.0 home.1
Async XLA Ops:
  0.6 18.7 %copy-start.2 = (bf16[1024,1,320]{0,2,1:T(8,128)(2,1)S(1)}, bf16[1024,1,320]{0,2,1:T(8,128)(2,1)}, u32[]{:S(2)}) copy-start(bf16[1024,1,320]{0,2,1:T(8,128)(2,1)} %param.13) | copy-start | bytes 1966084
  2.7 27.9 %all-to-all-start = ((bf16[32,40,128]{2,1,0:T(8,128)(2,1)}), bf16[32,40,128]{2,1,0:T(8,128)(2,1)S(1)}, u32[]{:S(2)}, u32[]{:S(2)}) async-start(bf16[32,40,128]{2,1,0:T(8,128)(2,1)} %pack.1), calls=%async_computation | async-start | bytes 655360 | tf_op jit(solution)/shard_map/all_to_all | solution.py:256
  19.4 1.1 copy-start.3
  20.5 10.1 %copy-start.4 = (bf16[1,1024,224]{1,2,0:T(8,128)(2,1)S(1)}, bf16[1,1024,224]{1,2,0:T(8,128)(2,1)}, u32[]{:S(2)}) copy-start(bf16[1,1024,224]{1,2,0:T(8,128)(2,1)} %param.17) | copy-start | bytes 1376260
  31.9 3.1 %copy-start.5 = (bf16[320,224]{1,0:T(8,128)(2,1)}, bf16[320,224]{1,0:T(8,128)(2,1)S(1)}, u32[]{:S(2)}) copy-start(bf16[320,224]{1,0:T(8,128)(2,1)S(1)} %get-tuple-element.49.x_ref) | copy-start | bytes 430084
  31.9 3.5 %collective-permute-start = (bf16[16,40,256]{2,1,0:T(8,128)(2,1)S(1)}, bf16[16,40,256]{2,1,0:T(8,128)(2,1)S(1)}, u32[]{:S(2)}, u32[]{:S(2)}) collective-permute-start(bf16[16,40,256]{2,1,0:T(8,128)(2,1)S(1)} %get-tuple-element.36), channel_id=1, source_target_pairs={{0,1},{1,0},{2,3},{3,2},{4,5},{5,4},{6,7},{7,6},{8,9},{9,8},{10,11... | collective-permute-start | bytes 983048 | tf_op jit(solution)/shard_map/ppermute | solution.py:273
  64.1 33.2 %copy-start.1 = (bf16[1,224,1024]{2,1,0:T(8,128)(2,1)S(1)}, bf16[1,224,1024]{2,1,0:T(8,128)(2,1)}, u32[]{:S(2)}) copy-start(bf16[1,224,1024]{2,1,0:T(8,128)(2,1)} %param.16) | copy-start | bytes 1376260
  64.1 33.1 %copy-start = (bf16[1,224,1024]{2,1,0:T(8,128)(2,1)S(1)}, bf16[1,224,1024]{2,1,0:T(8,128)(2,1)}, u32[]{:S(2)}) copy-start(bf16[1,224,1024]{2,1,0:T(8,128)(2,1)} %param.15) | copy-start | bytes 1376260
  85.5 13.0 %collective-permute-start.1 = (bf16[16,40,256]{2,1,0:T(8,128)(2,1)S(1)}, bf16[16,40,256]{2,1,0:T(8,128)(2,1)S(1)}, u32[]{:S(2)}, u32[]{:S(2)}) collective-permute-start(bf16[16,40,256]{2,1,0:T(8,128)(2,1)S(1)} %all_to_all.21.refs_0_), channel_id=1, source_target_pairs={{0,1},{1,0},{2,3},{3,2},{4,5},{5,4},{6,7},{7,6},{8,9},{9,8},{10,11... | collective-permute-start | bytes 983048 | tf_op jit(solution)/shard_map/ppermute | solution.py:281
  100.6 5.2 %copy-start.6 = (bf16[320,224]{1,0:T(8,128)(2,1)S(1)}, bf16[320,224]{1,0:T(8,128)(2,1)}, u32[]{:S(2)}) copy-start(bf16[320,224]{1,0:T(8,128)(2,1)} %copy-done.5) | copy-start | bytes 430084
  100.6 16.4 %all-to-all-start.3 = ((bf16[32,24,128]{2,1,0:T(8,128)(2,1)}), bf16[32,24,128]{2,1,0:T(8,128)(2,1)S(1)}, u32[]{:S(2)}, u32[]{:S(2)}) async-start(bf16[32,24,128]{2,1,0:T(8,128)(2,1)} %get-tuple-element.46), calls=%async_computation.3 | async-start | bytes 393216 | tf_op jit(solution)/shard_map/all_to_all | solution.py:295
  105.7 11.3 %copy-start.7 = (s32[32,8]{0,1:T(8,128)S(1)}, s32[32,8]{0,1:T(8,128)}, u32[]{:S(2)}) copy-start(s32[32,8]{0,1:T(8,128)} %param.12) | copy-start | bytes 3076

commit v4 on v3

--- a/solution.py
+++ b/solution.py
@@ -15,7 +15,7 @@
 SLOTS = 320
 PACK = 40
 HOME = 24
-STAGGER = 9000
+STAGGER = 8000
 TP = ("tp_0", "tp_1")
 EP = ("ex", "ey")
 F32 = jnp.float32
@@ -49,7 +49,12 @@
     return jnp.where(named > 0.5, place, -1.0), weight
 
 
-def pack_kernel(ids_ref, gates_ref, tok_ref, cot_ref, out_ref):
+def quarter(block_ref, out_ref, done, j):
+    rows = pl.ds(8 * j, 8)
+    return pltpu.make_async_copy(block_ref.at[rows], out_ref.at[rows], done.at[j])
+
+
+def pack_kernel(ids_ref, gates_ref, tok_ref, cot_ref, out_ref, block_ref, done):
     place, weight = places(ids_ref[...], gates_ref[...].astype(F32))
     place = jnp.concatenate([place] * 4, axis=1)
     weight = jnp.concatenate([weight] * 4, axis=1)
@@ -78,11 +83,25 @@
         picks.append(jnp.concatenate([pick, gate], axis=1))
     for j in range(4):
         part = jnp.concatenate(picks[8 * j : 8 * j + 8], axis=0).astype(BF16)
-        out_ref[8 * j : 8 * j + 8] = dot(part, source).astype(BF16).reshape(8, PACK, 128)
-
-
-def product_kernel(core_ref, recv_ref, down_ref, kept_ref, given_ref, x_ref, scaled_ref, gate_ref):
-    core = core_ref[0]
+        block_ref[8 * j : 8 * j + 8] = dot(part, source).astype(BF16).reshape(8, PACK, 128)
+        quarter(block_ref, out_ref, done, j).start()
+    for j in range(4):
+        quarter(block_ref, out_ref, done, j).wait()
+
+
+def half_product(dy, first, down_ref, out_ref):
+    part = dot(dy, jnp.where(first, down_ref[:, :512], down_ref[:, 512:]))
+    for v in range(2):
+        for b in range(8):
+            out_ref[8 * v + b] = part[40 * b : 40 * b + 40, 256 * v : 256 * v + 256].astype(BF16)
+
+
+def kept_kernel(core_ref, dy_ref, down_ref, scaled_ref, hidden_ref, kept_ref, wd_ref):
+    half_product(dy_ref[...], core_ref[0] == 0, down_ref, kept_ref)
+    wd_ref[...] = dot(scaled_ref[...], hidden_ref[...], OVER_ROWS).astype(BF16)
+
+
+def product_kernel(core_ref, recv_ref, down_ref, given_ref, dy_ref, x_ref, scaled_ref, gate_ref):
     to_x = jnp.concatenate([iota((128, 128), 1), iota((128, 128), 1)], axis=0)
     at = iota((256, 128), 0)
     from_x = jnp.where(to_x < 64, to_x, to_x + 64)
@@ -94,7 +113,6 @@
     slot, place = iota((8 * CAP, 8 * PACK), 0), iota((8 * CAP, 8 * PACK), 1)
     base = (slot // CAP) * PACK + slot % CAP
     picks = [jnp.where(place == base + CAP * kind, 1.0, 0.0).astype(BF16) for kind in range(4)]
-    dys = []
     for j in range(4):
         got = recv_ref[8 * j : 8 * j + 8].reshape(8 * PACK, 128)
         x_low, dy_low, middle, last = [dot(pick, got) for pick in picks]
@@ -108,14 +126,8 @@
         x_ref[rows, :] = x.astype(BF16)
         scaled_ref[rows, :] = (gate * dy).astype(BF16)
         gate_ref[rows, :] = jnp.broadcast_to(gate, (8 * CAP, 128))
-        dys.append(dy.astype(BF16))
-    dy = jnp.concatenate(dys, axis=0)
-    low, high = down_ref[:, :512], down_ref[:, 512:]
-    for ref, first in ((given_ref, core == 1), (kept_ref, core == 0)):
-        part = dot(dy, jnp.where(first, low, high))
-        for v in range(2):
-            for b in range(8):
-                ref[8 * v + b] = part[40 * b : 40 * b + 40, 256 * v : 256 * v + 256].astype(BF16)
+        dy_ref[rows, :] = dy.astype(BF16)
+    half_product(dy_ref[...], core_ref[0] == 1, down_ref, given_ref)
 
 
 def factors_kernel(gate_ref, up_ref, hidden_ref, by_gate_ref, by_up_ref):
@@ -130,10 +142,6 @@
         by_up_ref[rows, :] = by_up.astype(BF16)
 
 
-def down_kernel(scaled_ref, hidden_ref, wd_ref):
-    wd_ref[...] = dot(scaled_ref[...], hidden_ref[...], OVER_ROWS).astype(BF16)
-
-
 def weights_kernel(core_ref, x_ref, own_dg_ref, own_du_ref, dg_ref, du_ref, wg_ref, wu_ref):
     core = core_ref[0]
     for half, dg, du in ((core, own_dg_ref, own_du_ref), (1 - core, dg_ref, du_ref)):
@@ -160,7 +168,7 @@
         copies_ref[z] = total
 
 
-def half_grads(half, half_ref, gate_ref, by_gate_ref, by_up_ref, hidden_ref, wg_ref, wu_ref, dg_out, du_out, dx_ref, dg_ref, du_ref, done, first):
+def half_grads(half, half_ref, gate_ref, by_gate_ref, by_up_ref, hidden_ref, wg_ref, wu_ref, before_ref, dg_out, du_out, dx_ref, dg_ref, du_ref, done):
     for b in range(8):
         rows = slice(40 * b, 40 * b + 40)
         gate = gate_ref[rows, 0:1]
@@ -174,25 +182,24 @@
             du_ref[rows, here] = (dh * by_up_ref[rows, units].astype(F32)).astype(BF16)
             score = score + jnp.sum(total * hidden_ref[rows, units].astype(F32), axis=1, keepdims=True)
         score = jnp.broadcast_to(score, (40, 256 - WIDTH))
-        dx_ref[rows, WIDTH:] = score if first else dx_ref[rows, WIDTH:] + score
+        dx_ref[rows, WIDTH:] = score if before_ref is None else before_ref[rows, WIDTH:] + score
     copies = [pltpu.make_async_copy(dg_ref, dg_out, done.at[0]), pltpu.make_async_copy(du_ref, du_out, done.at[1])]
     for copy in copies:
         copy.start()
     units = pl.ds(pl.multiple_of(512 * half, 512), 512)
     dx = dot(dg_ref[...], wg_ref[:, units], OVER_UNITS) + dot(du_ref[...], wu_ref[:, units], OVER_UNITS)
-    dx_ref[:, :WIDTH] = dx if first else dx_ref[:, :WIDTH] + dx
+    dx_ref[:, :WIDTH] = dx if before_ref is None else before_ref[:, :WIDTH] + dx
     return copies
 
 
 def own_kernel(core_ref, *refs):
-    for copy in half_grads(core_ref[0], *refs, True):
+    for copy in half_grads(core_ref[0], *refs[:7], None, *refs[7:]):
         copy.wait()
 
 
 def other_kernel(core_ref, *refs):
-    shared, own_ref, dg_out, du_out, back_ref, dx_ref, scratch = refs[:7], *refs[7:12], refs[12:]
-    dx_ref[...] = own_ref[...]
-    copies = half_grads(1 - core_ref[0], *shared, dg_out, du_out, dx_ref, *scratch, False)
+    given, dg_out, du_out, out_ref, back_ref, sent, dx_ref, scratch = refs[:8], *refs[8:14], refs[14:]
+    copies = half_grads(1 - core_ref[0], *given, dg_out, du_out, dx_ref, *scratch)
     out, row = iota((8 * HOME, 8 * CAP), 0), iota((8 * HOME, 8 * CAP), 1)
     block, place = out // HOME, out % HOME
     same = row // CAP == block
@@ -202,7 +209,8 @@
         rows = slice(8 * CAP * j, 8 * CAP * (j + 1))
         spread = dot(low, dx_ref[rows, :128].astype(BF16)) + dot(high, dx_ref[rows, 128:].astype(BF16))
         back_ref[8 * j : 8 * j + 8] = spread.astype(BF16).reshape(8, HOME, 128)
-    for copy in copies:
+        quarter(back_ref, out_ref, sent, j).start()
+    for copy in copies + [quarter(back_ref, out_ref, sent, j) for j in range(4)]:
         copy.wait()
 
 
@@ -251,7 +259,8 @@
     chips = lax.axis_size("tp_0")
     pairs = [(2 * z + c, 2 * z + 1 - c) for z in range(chips) for c in range(2)]
     send = call(
-        pack_kernel, [((EXPERTS, PACK, 128), BF16, False)], [ids, gates.T, tokens, cotangent], name="pack", room=60
+        pack_kernel, [((EXPERTS, PACK, 128), BF16, None)], [ids, gates.T, tokens, cotangent],
+        [pltpu.VMEM((EXPERTS, PACK, 128), BF16), pltpu.SemaphoreType.DMA((4,))], name="pack", room=60,
     )[0]
     recv = lax.all_to_all(send, EP, 0, 0, tiled=True)
     units = ((SLOTS, UNITS), BF16, True)
@@ -263,16 +272,20 @@
     )
     recv, hidden, by_gate, by_up = lax.optimization_barrier((recv, hidden, by_gate, by_up))
     half = ((chips, 40, 256), BF16, True)
-    kept, given, x, scaled, gate = call(
+    rows = ((SLOTS, WIDTH), BF16, True)
+    down = near(w_down[0].T)
+    given, dy, x, scaled, gate = call(
         product_kernel,
-        [half, half, ((SLOTS, WIDTH), BF16, False), ((SLOTS, WIDTH), BF16, True), ((SLOTS, 128), F32, True)],
-        [core, near(recv), near(w_down[0].T)],
+        [half, rows, ((SLOTS, WIDTH), BF16, False), rows, ((SLOTS, 128), F32, True)],
+        [core, near(recv), down],
         name="product",
     )
     weights = ((WIDTH, UNITS), BF16, False)
     got = lax.ppermute(given, TP, pairs)
-    grad_w_down = call(down_kernel, [weights], [near(scaled), near(hidden)], name="down")[0]
-    got, grad_w_down = lax.optimization_barrier((got, grad_w_down))
+    kept, grad_w_down = call(
+        kept_kernel, [half, weights], [core, near(dy), down, near(scaled), near(hidden)], name="kept"
+    )
+    got, kept = lax.optimization_barrier((got, kept))
     pair = call(pair_kernel, [half], [core, near(kept), near(got)], name="pair")[0]
     terms = lax.all_to_all(pair, "tp_0", 0, 0, tiled=True)
 
@@ -287,9 +300,14 @@
     other, own_dx = lax.optimization_barrier((other, own_dx))
     dg, du, back = call(
         other_kernel,
-        [wide_half, wide_half, ((EXPERTS, HOME, 128), BF16, False)],
+        [wide_half, wide_half, ((EXPERTS, HOME, 128), BF16, None)],
         [core, near(other), *shared, near(own_dx)],
-        scratch=[pltpu.VMEM((SLOTS, 256), F32), *drafts],
+        scratch=[
+            pltpu.VMEM((EXPERTS, HOME, 128), BF16),
+            pltpu.SemaphoreType.DMA((4,)),
+            pltpu.VMEM((SLOTS, 256), F32),
+            *drafts,
+        ],
         name="other",
     )
     home = lax.all_to_all(back, EP, 0, 0, tiled=True)

time: 119 us -> 117 us (0.983)
  starting transfers between devices: 35.4 us -> 33.4 us
    ppermute x1, starting transfers between devices: 11.7 us -> 9.81 us  [on_device(): other = lax.ppermute(own, TP, pairs)]
where the time goes in v4:
time: 117 us
  blocking collectives  50.6 us (43%)
  starting transfers between devices  33.4 us (29%)
  waiting for transfers between devices  19.9 us (17%)
  Pallas kernels  10.8 us (9%)
    all_to_all x1, blocking collectives, on_device(): terms = lax.all_to_all(pair, 'tp_0', 0, 0, tiled=True)  28.6 us
    all_to_all x1, blocking collectives, on_device(): own = lax.all_to_all(copies, 'tp_0', 0, 0, tiled=True)  22.1 us
    all_to_all x1, starting transfers between devices, on_device(): recv = lax.all_to_all(send, EP, 0, 0, tiled=True)  16.6 us
    pallas_call x10, Pallas kernels, call(): pl.pallas_call(body, out_shape=[pltpu.VMEM(shape, dtype) if stays else ja...  10.8 us
    all_to_all x1, waiting for transfers between devices, on_device(): home = lax.all_to_all(back, EP, 0, 0, tiled=True)  9.82 us
    ppermute x1, starting transfers between devices, on_device(): other = lax.ppermute(own, TP, pairs)  9.81 us
    all_to_all x1, waiting for transfers between devices, on_device(): recv = lax.all_to_all(send, EP, 0, 0, tiled=True)  9.46 us
    all_to_all x1, starting transfers between devices, on_device(): home = lax.all_to_all(back, EP, 0, 0, tiled=True)  5.05 us
  transfers between devices with their start and end apart: 4, of which 4 were waited for; matrix products, arithmetic and copies ran while one was open for 0% of the time, Pallas kernels for 4%

profile of v4, /device:TPU:8, one launch (start us, length us, event | category | flops | bytes accessed | tf_op | source)
XLA Modules:
  0.0 116.6 jit_solution(1831343293940764265)
XLA Ops:
  0.6 0.0 copy-start.3
  0.6 2.0 %pack.1 = bf16[32,40,128]{2,1,0:T(8,128)(2,1)} custom-call(s32[8,32]{1,0:T(8,128)} %bitcast.28, bf16[8,32]{1,0:T(8,128)(2,1)} %bitcast.30, bf16[32,224]{1,0:T(8,128)(2,1)} %tok_ref.1, bf16[32,224]{1,0:T(8,128)(2,1)} %cot_ref.1), custom_call_target="tpu_custom_call" | custom-call | tf_op jit(solution)/shard_map/pack/pallas_call | solution.py:242
  2.7 16.6 %all-to-all-start = ((bf16[32,40,128]{2,1,0:T(8,128)(2,1)}), bf16[32,40,128]{2,1,0:T(8,128)(2,1)S(1)}, u32[]{:S(2)}, u32[]{:S(2)}) async-start(bf16[32,40,128]{2,1,0:T(8,128)(2,1)} %pack.1), calls=%async_computation | async-start | bytes 655360 | tf_op jit(solution)/shard_map/all_to_all | solution.py:265
  19.3 0.0 copy-done.3
  19.3 0.0 copy-start.4
  19.4 1.1 copy-done.4
  20.4 0.0 copy-start
  20.4 0.7 factors.1
  21.1 9.5 %all-to-all-done.recv_ref = bf16[32,40,128]{2,1,0:T(8,128)(2,1)S(1)} async-done(((bf16[32,40,128]{2,1,0:T(8,128)(2,1)}), bf16[32,40,128]{2,1,0:T(8,128)(2,1)S(1)}, u32[]{:S(2)}, u32[]{:S(2)}) %all-to-all-start) | async-done | bytes 327712 | tf_op jit(solution)/shard_map/all_to_all | solution.py:265
  30.6 0.0 copy-done
  30.6 1.2 %product.1 = (bf16[16,40,256]{2,1,0:T(8,128)(2,1)S(1)}, bf16[320,224]{1,0:T(8,128)(2,1)S(1)}, bf16[320,224]{1,0:T(8,128)(2,1)S(1)}, bf16[320,224]{1,0:T(8,128)(2,1)S(1)}, f32[320,128]{1,0:T(8,128)S(1)}) custom-call(s32[1]{0:T(128)} %bitcast.1.core_ref, bf16[32,40,128]{2,1,0:T(8,128)(2,1)S(1)} %all-to-all-done.recv_ref, bf16[224,1024]{1,0:T(8,128)(2,1)S(1)} %bitcast.20), custom_call_target="tpu_custom_call" | custom-call | tf_op jit(solution)/shard_map/product/pallas_call | solution.py:242
  31.8 1.9 %collective-permute-start = (bf16[16,40,256]{2,1,0:T(8,128)(2,1)S(1)}, bf16[16,40,256]{2,1,0:T(8,128)(2,1)S(1)}, u32[]{:S(2)}, u32[]{:S(2)}) collective-permute-start(bf16[16,40,256]{2,1,0:T(8,128)(2,1)S(1)} %get-tuple-element.37), channel_id=1, source_target_pairs={{0,1},{1,0},{2,3},{3,2},{4,5},{5,4},{6,7},{7,6},{8,9},{9,8},{10,11... | collective-permute-start | bytes 983048 | tf_op jit(solution)/shard_map/ppermute | solution.py:284
  33.7 1.3 %kept.1 = (bf16[16,40,256]{2,1,0:T(8,128)(2,1)S(1)}, bf16[224,1024]{1,0:T(8,128)(2,1)}) custom-call(s32[1]{0:T(128)} %bitcast.1.core_ref, bf16[320,224]{1,0:T(8,128)(2,1)S(1)} %get-tuple-element.38.dy_ref, bf16[224,1024]{1,0:T(8,128)(2,1)S(1)} %bitcast.21, bf16[320,224]{1,0:T(8,128)(2,1)S(1)} %get-tuple-element.39.scaled_ref, ...), custom_call_target="tpu_custom_call" | custom-call | tf_op jit(solution)/shard_map/kept/pallas_call | solution.py:242
  35.0 0.3 collective-permute-done.got_ref
  35.3 0.1 pair.1
  35.4 28.6 %all_to_all.20.terms_ref = bf16[16,40,256]{2,1,0:T(8,128)(2,1)S(1)} all-to-all(bf16[16,40,256]{2,1,0:T(8,128)(2,1)S(1)} %pair.1), channel_id=1, replica_groups=mesh['ex'=8,'ey'=4,'tp_0'=16,'tp_1'=2] {'tp_0'}, dimensions={0} | all-to-all | bytes 655360 | tf_op jit(solution)/shard_map/all_to_all | solution.py:290
  64.0 0.0 copy-start.2
  64.0 0.1 spread.1
  64.0 0.0 copy-start.1
  64.0 22.1 %all_to_all.21.refs_0_ = bf16[16,40,256]{2,1,0:T(8,128)(2,1)S(1)} all-to-all(bf16[16,40,256]{2,1,0:T(8,128)(2,1)S(1)} %spread.1), channel_id=1, replica_groups=mesh['ex'=8,'ey'=4,'tp_0'=16,'tp_1'=2] {'tp_0'}, dimensions={0} | all-to-all | bytes 655360 | tf_op jit(solution)/shard_map/all_to_all | solution.py:293
  86.1 9.8 %collective-permute-start.1 = (bf16[16,40,256]{2,1,0:T(8,128)(2,1)S(1)}, bf16[16,40,256]{2,1,0:T(8,128)(2,1)S(1)}, u32[]{:S(2)}, u32[]{:S(2)}) collective-permute-start(bf16[16,40,256]{2,1,0:T(8,128)(2,1)S(1)} %all_to_all.21.refs_0_), channel_id=1, source_target_pairs={{0,1},{1,0},{2,3},{3,2},{4,5},{5,4},{6,7},{7,6},{8,9},{9,8},{10,11... | collective-permute-start | bytes 983048 | tf_op jit(solution)/shard_map/ppermute | solution.py:294
  95.9 0.0 copy-done.2
  95.9 0.0 copy-done.1
  95.9 0.9 own.1
  96.9 0.3 collective-permute-done.1.refs_0_
  97.2 2.0 %other.1 = (bf16[320,512]{1,0:T(8,128)(2,1)S(1)}, bf16[320,512]{1,0:T(8,128)(2,1)S(1)}, bf16[32,24,128]{2,1,0:T(8,128)(2,1)}) custom-call(s32[1]{0:T(128)} %bitcast.1.core_ref, bf16[16,40,256]{2,1,0:T(8,128)(2,1)S(1)} %collective-permute-done.1.refs_0_, f32[320,128]{1,0:T(8,128)S(1)} %get-tuple-element.44.refs_1_, ...), custom_call_target="tpu_custom_call" | custom-call | tf_op jit(solution)/shard_map/other/pallas_call | solution.py:242
  99.2 5.0 %all-to-all-start.3 = ((bf16[32,24,128]{2,1,0:T(8,128)(2,1)}), bf16[32,24,128]{2,1,0:T(8,128)(2,1)S(1)}, u32[]{:S(2)}, u32[]{:S(2)}) async-start(bf16[32,24,128]{2,1,0:T(8,128)(2,1)} %get-tuple-element.50), calls=%async_computation.3 | async-start | bytes 393216 | tf_op jit(solution)/shard_map/all_to_all | solution.py:313
  104.2 0.0 copy-start.5
  104.2 1.5 %weights.1 = (bf16[224,1024]{1,0:T(8,128)(2,1)}, bf16[224,1024]{1,0:T(8,128)(2,1)}) custom-call(s32[1]{0:T(128)} %bitcast.1.core_ref, bf16[320,224]{1,0:T(8,128)(2,1)S(1)} %get-tuple-element.53.x_ref, bf16[320,512]{1,0:T(8,128)(2,1)S(1)} %get-tuple-element.54.own_dg_ref, bf16[320,512]{1,0:T(8,128)(2,1)S(1)} %get-tuple-element.55.own_du_ref, ...), custom_call_target="tpu_custom_call" | custom-call | tf_op jit(solution)/shard_map/weights/pallas_call | solution.py:242
  105.7 9.8 %all-to-all-done.3.home_ref = bf16[32,24,128]{2,1,0:T(8,128)(2,1)S(1)} async-done(((bf16[32,24,128]{2,1,0:T(8,128)(2,1)}), bf16[32,24,128]{2,1,0:T(8,128)(2,1)S(1)}, u32[]{:S(2)}, u32[]{:S(2)}) %all-to-all-start.3) | async-done | bytes 196640 | tf_op jit(solution)/shard_map/all_to_all | solution.py:313
  115.5 0.0 copy-done.5
  115.5 1.0 home.1
Async XLA Ops:
  0.6 18.7 %copy-start.3 = (bf16[1024,1,320]{0,2,1:T(8,128)(2,1)S(1)}, bf16[1024,1,320]{0,2,1:T(8,128)(2,1)}, u32[]{:S(2)}) copy-start(bf16[1024,1,320]{0,2,1:T(8,128)(2,1)} %param.13) | copy-start | bytes 1966084
  2.7 27.9 %all-to-all-start = ((bf16[32,40,128]{2,1,0:T(8,128)(2,1)}), bf16[32,40,128]{2,1,0:T(8,128)(2,1)S(1)}, u32[]{:S(2)}, u32[]{:S(2)}) async-start(bf16[32,40,128]{2,1,0:T(8,128)(2,1)} %pack.1), calls=%async_computation | async-start | bytes 655360 | tf_op jit(solution)/shard_map/all_to_all | solution.py:265
  19.3 1.1 copy-start.4
  20.4 10.1 %copy-start = (bf16[1,1024,224]{1,2,0:T(8,128)(2,1)S(1)}, bf16[1,1024,224]{1,2,0:T(8,128)(2,1)}, u32[]{:S(2)}) copy-start(bf16[1,1024,224]{1,2,0:T(8,128)(2,1)} %param.17) | copy-start | bytes 1376260
  31.8 3.5 %collective-permute-start = (bf16[16,40,256]{2,1,0:T(8,128)(2,1)S(1)}, bf16[16,40,256]{2,1,0:T(8,128)(2,1)S(1)}, u32[]{:S(2)}, u32[]{:S(2)}) collective-permute-start(bf16[16,40,256]{2,1,0:T(8,128)(2,1)S(1)} %get-tuple-element.37), channel_id=1, source_target_pairs={{0,1},{1,0},{2,3},{3,2},{4,5},{5,4},{6,7},{7,6},{8,9},{9,8},{10,11... | collective-permute-start | bytes 983048 | tf_op jit(solution)/shard_map/ppermute | solution.py:284
  64.0 32.0 %copy-start.2 = (bf16[1,224,1024]{2,1,0:T(8,128)(2,1)S(1)}, bf16[1,224,1024]{2,1,0:T(8,128)(2,1)}, u32[]{:S(2)}) copy-start(bf16[1,224,1024]{2,1,0:T(8,128)(2,1)} %param.16) | copy-start | bytes 1376260
  64.0 31.9 %copy-start.1 = (bf16[1,224,1024]{2,1,0:T(8,128)(2,1)S(1)}, bf16[1,224,1024]{2,1,0:T(8,128)(2,1)}, u32[]{:S(2)}) copy-start(bf16[1,224,1024]{2,1,0:T(8,128)(2,1)} %param.15) | copy-start | bytes 1376260
  86.1 11.0 %collective-permute-start.1 = (bf16[16,40,256]{2,1,0:T(8,128)(2,1)S(1)}, bf16[16,40,256]{2,1,0:T(8,128)(2,1)S(1)}, u32[]{:S(2)}, u32[]{:S(2)}) collective-permute-start(bf16[16,40,256]{2,1,0:T(8,128)(2,1)S(1)} %all_to_all.21.refs_0_), channel_id=1, source_target_pairs={{0,1},{1,0},{2,3},{3,2},{4,5},{5,4},{6,7},{7,6},{8,9},{9,8},{10,11... | collective-permute-start | bytes 983048 | tf_op jit(solution)/shard_map/ppermute | solution.py:294
  99.2 16.4 %all-to-all-start.3 = ((bf16[32,24,128]{2,1,0:T(8,128)(2,1)}), bf16[32,24,128]{2,1,0:T(8,128)(2,1)S(1)}, u32[]{:S(2)}, u32[]{:S(2)}) async-start(bf16[32,24,128]{2,1,0:T(8,128)(2,1)} %get-tuple-element.50), calls=%async_computation.3 | async-start | bytes 393216 | tf_op jit(solution)/shard_map/all_to_all | solution.py:313
  104.2 11.3 %copy-start.5 = (s32[32,8]{0,1:T(8,128)S(1)}, s32[32,8]{0,1:T(8,128)}, u32[]{:S(2)}) copy-start(s32[32,8]{0,1:T(8,128)} %param.12) | copy-start | bytes 3076

commit v5 on v4

--- a/solution.py
+++ b/solution.py
@@ -15,7 +15,7 @@
 SLOTS = 320
 PACK = 40
 HOME = 24
-STAGGER = 8000
+STAGGER = 6500
 TP = ("tp_0", "tp_1")
 EP = ("ex", "ey")
 F32 = jnp.float32
@@ -151,7 +151,7 @@
 
 
 def pair_kernel(core_ref, kept_ref, got_ref, pair_ref):
-    @pl.when(core_ref[0] == 1)
+    @pl.when(core_ref[0] == 0)
     def _():
         pl.delay(STAGGER)
 

time: 117 us -> 116 us (level)
  the two profiles are of different devices: /device:TPU:8 before, /device:TPU:72 now
where the time goes in v5:
time: 116 us; the launch traced here: 115 us
  blocking collectives  55.2 us (48%)
  waiting for transfers between devices  22 us (19%)
  starting transfers between devices  19 us (16%)
  Pallas kernels  17.2 us (15%)
    all_to_all x1, blocking collectives, on_device(): terms = lax.all_to_all(pair, 'tp_0', 0, 0, tiled=True)  34.1 us
    all_to_all x1, blocking collectives, on_device(): own = lax.all_to_all(copies, 'tp_0', 0, 0, tiled=True)  21.1 us
    pallas_call x10, Pallas kernels, call(): pl.pallas_call(body, out_shape=[pltpu.VMEM(shape, dtype) if stays else ja...  17.2 us
    all_to_all x1, waiting for transfers between devices, on_device(): recv = lax.all_to_all(send, EP, 0, 0, tiled=True)  11.5 us
    all_to_all x1, starting transfers between devices, on_device(): recv = lax.all_to_all(send, EP, 0, 0, tiled=True)  10.2 us
    all_to_all x1, waiting for transfers between devices, on_device(): home = lax.all_to_all(back, EP, 0, 0, tiled=True)  9.59 us
    all_to_all x1, starting transfers between devices, on_device(): home = lax.all_to_all(back, EP, 0, 0, tiled=True)  5.04 us
  transfers between devices with their start and end apart: 4, of which 4 were waited for; matrix products, arithmetic and copies ran while one was open for 0% of the time, Pallas kernels for 4%

profile of v5, /device:TPU:72, one launch (start us, length us, event | category | flops | bytes accessed | tf_op | source)
XLA Modules:
  0.0 115.4 jit_solution(13807266951228908191)
XLA Ops:
  0.6 0.0 copy-start.3
  0.6 2.0 %pack.1 = bf16[32,40,128]{2,1,0:T(8,128)(2,1)} custom-call(s32[8,32]{1,0:T(8,128)} %bitcast.28, bf16[8,32]{1,0:T(8,128)(2,1)} %bitcast.30, bf16[32,224]{1,0:T(8,128)(2,1)} %tok_ref.1, bf16[32,224]{1,0:T(8,128)(2,1)} %cot_ref.1), custom_call_target="tpu_custom_call" | custom-call | tf_op jit(solution)/shard_map/pack/pallas_call | solution.py:242
  2.7 10.2 %all-to-all-start = ((bf16[32,40,128]{2,1,0:T(8,128)(2,1)}), bf16[32,40,128]{2,1,0:T(8,128)(2,1)S(1)}, u32[]{:S(2)}, u32[]{:S(2)}) async-start(bf16[32,40,128]{2,1,0:T(8,128)(2,1)} %pack.1), calls=%async_computation | async-start | bytes 655360 | tf_op jit(solution)/shard_map/all_to_all | solution.py:265
  12.9 0.0 copy-done.3
  12.9 0.0 copy-start.4
  12.9 1.1 copy-done.4
  14.0 0.0 copy-start
  14.0 0.7 factors.1
  14.6 11.5 %all-to-all-done.recv_ref = bf16[32,40,128]{2,1,0:T(8,128)(2,1)S(1)} async-done(((bf16[32,40,128]{2,1,0:T(8,128)(2,1)}), bf16[32,40,128]{2,1,0:T(8,128)(2,1)S(1)}, u32[]{:S(2)}, u32[]{:S(2)}) %all-to-all-start) | async-done | bytes 327712 | tf_op jit(solution)/shard_map/all_to_all | solution.py:265
  26.1 0.0 copy-done
  26.1 1.2 %product.1 = (bf16[16,40,256]{2,1,0:T(8,128)(2,1)S(1)}, bf16[320,224]{1,0:T(8,128)(2,1)S(1)}, bf16[320,224]{1,0:T(8,128)(2,1)S(1)}, bf16[320,224]{1,0:T(8,128)(2,1)S(1)}, f32[320,128]{1,0:T(8,128)S(1)}) custom-call(s32[1]{0:T(128)} %bitcast.1.core_ref, bf16[32,40,128]{2,1,0:T(8,128)(2,1)S(1)} %all-to-all-done.recv_ref, bf16[224,1024]{1,0:T(8,128)(2,1)S(1)} %bitcast.20), custom_call_target="tpu_custom_call" | custom-call | tf_op jit(solution)/shard_map/product/pallas_call | solution.py:242
  27.3 1.9 %collective-permute-start = (bf16[16,40,256]{2,1,0:T(8,128)(2,1)S(1)}, bf16[16,40,256]{2,1,0:T(8,128)(2,1)S(1)}, u32[]{:S(2)}, u32[]{:S(2)}) collective-permute-start(bf16[16,40,256]{2,1,0:T(8,128)(2,1)S(1)} %get-tuple-element.37), channel_id=1, source_target_pairs={{0,1},{1,0},{2,3},{3,2},{4,5},{5,4},{6,7},{7,6},{8,9},{9,8},{10,11... | collective-permute-start | bytes 983048 | tf_op jit(solution)/shard_map/ppermute | solution.py:284
  29.3 1.3 %kept.1 = (bf16[16,40,256]{2,1,0:T(8,128)(2,1)S(1)}, bf16[224,1024]{1,0:T(8,128)(2,1)}) custom-call(s32[1]{0:T(128)} %bitcast.1.core_ref, bf16[320,224]{1,0:T(8,128)(2,1)S(1)} %get-tuple-element.38.dy_ref, bf16[224,1024]{1,0:T(8,128)(2,1)S(1)} %bitcast.21, bf16[320,224]{1,0:T(8,128)(2,1)S(1)} %get-tuple-element.39.scaled_ref, ...), custom_call_target="tpu_custom_call" | custom-call | tf_op jit(solution)/shard_map/kept/pallas_call | solution.py:242
  30.5 0.3 collective-permute-done.got_ref
  30.9 6.6 %pair.1 = bf16[16,40,256]{2,1,0:T(8,128)(2,1)S(1)} custom-call(s32[1]{0:T(128)} %bitcast.1.core_ref, bf16[16,40,256]{2,1,0:T(8,128)(2,1)S(1)} %get-tuple-element.42.kept_ref, bf16[16,40,256]{2,1,0:T(8,128)(2,1)S(1)} %collective-permute-done.got_ref), custom_call_target="tpu_custom_call" | custom-call | tf_op jit(solution)/shard_map/pair/pallas_call | solution.py:242
  37.4 34.1 %all_to_all.20.terms_ref = bf16[16,40,256]{2,1,0:T(8,128)(2,1)S(1)} all-to-all(bf16[16,40,256]{2,1,0:T(8,128)(2,1)S(1)} %pair.1), channel_id=1, replica_groups=mesh['ex'=8,'ey'=4,'tp_0'=16,'tp_1'=2] {'tp_0'}, dimensions={0} | all-to-all | bytes 655360 | tf_op jit(solution)/shard_map/all_to_all | solution.py:290
  71.5 0.0 copy-start.2
  71.5 0.1 spread.1
  71.6 0.0 copy-start.1
  71.6 21.1 %all_to_all.21.refs_0_ = bf16[16,40,256]{2,1,0:T(8,128)(2,1)S(1)} all-to-all(bf16[16,40,256]{2,1,0:T(8,128)(2,1)S(1)} %spread.1), channel_id=1, replica_groups=mesh['ex'=8,'ey'=4,'tp_0'=16,'tp_1'=2] {'tp_0'}, dimensions={0} | all-to-all | bytes 655360 | tf_op jit(solution)/shard_map/all_to_all | solution.py:293
  92.7 1.9 %collective-permute-start.1 = (bf16[16,40,256]{2,1,0:T(8,128)(2,1)S(1)}, bf16[16,40,256]{2,1,0:T(8,128)(2,1)S(1)}, u32[]{:S(2)}, u32[]{:S(2)}) collective-permute-start(bf16[16,40,256]{2,1,0:T(8,128)(2,1)S(1)} %all_to_all.21.refs_0_), channel_id=1, source_target_pairs={{0,1},{1,0},{2,3},{3,2},{4,5},{5,4},{6,7},{7,6},{8,9},{9,8},{10,11... | collective-permute-start | bytes 983048 | tf_op jit(solution)/shard_map/ppermute | solution.py:294
  94.6 0.0 copy-done.2
  94.6 0.0 copy-done.1
  94.6 0.9 own.1
  95.6 0.6 collective-permute-done.1.refs_0_
  96.2 2.0 %other.1 = (bf16[320,512]{1,0:T(8,128)(2,1)S(1)}, bf16[320,512]{1,0:T(8,128)(2,1)S(1)}, bf16[32,24,128]{2,1,0:T(8,128)(2,1)}) custom-call(s32[1]{0:T(128)} %bitcast.1.core_ref, bf16[16,40,256]{2,1,0:T(8,128)(2,1)S(1)} %collective-permute-done.1.refs_0_, f32[320,128]{1,0:T(8,128)S(1)} %get-tuple-element.44.refs_1_, ...), custom_call_target="tpu_custom_call" | custom-call | tf_op jit(solution)/shard_map/other/pallas_call | solution.py:242
  98.2 5.0 %all-to-all-start.3 = ((bf16[32,24,128]{2,1,0:T(8,128)(2,1)}), bf16[32,24,128]{2,1,0:T(8,128)(2,1)S(1)}, u32[]{:S(2)}, u32[]{:S(2)}) async-start(bf16[32,24,128]{2,1,0:T(8,128)(2,1)} %get-tuple-element.50), calls=%async_computation.3 | async-start | bytes 393216 | tf_op jit(solution)/shard_map/all_to_all | solution.py:313
  103.3 0.0 copy-start.5
  103.3 1.5 %weights.1 = (bf16[224,1024]{1,0:T(8,128)(2,1)}, bf16[224,1024]{1,0:T(8,128)(2,1)}) custom-call(s32[1]{0:T(128)} %bitcast.1.core_ref, bf16[320,224]{1,0:T(8,128)(2,1)S(1)} %get-tuple-element.53.x_ref, bf16[320,512]{1,0:T(8,128)(2,1)S(1)} %get-tuple-element.54.own_dg_ref, bf16[320,512]{1,0:T(8,128)(2,1)S(1)} %get-tuple-element.55.own_du_ref, ...), custom_call_target="tpu_custom_call" | custom-call | tf_op jit(solution)/shard_map/weights/pallas_call | solution.py:242
  104.8 9.6 %all-to-all-done.3.home_ref = bf16[32,24,128]{2,1,0:T(8,128)(2,1)S(1)} async-done(((bf16[32,24,128]{2,1,0:T(8,128)(2,1)}), bf16[32,24,128]{2,1,0:T(8,128)(2,1)S(1)}, u32[]{:S(2)}, u32[]{:S(2)}) %all-to-all-start.3) | async-done | bytes 196640 | tf_op jit(solution)/shard_map/all_to_all | solution.py:313
  114.3 0.0 copy-done.5
  114.3 1.0 home.1
Async XLA Ops:
  0.6 12.3 %copy-start.3 = (bf16[1024,1,320]{0,2,1:T(8,128)(2,1)S(1)}, bf16[1024,1,320]{0,2,1:T(8,128)(2,1)}, u32[]{:S(2)}) copy-start(bf16[1024,1,320]{0,2,1:T(8,128)(2,1)} %param.13) | copy-start | bytes 1966084
  2.7 23.4 %all-to-all-start = ((bf16[32,40,128]{2,1,0:T(8,128)(2,1)}), bf16[32,40,128]{2,1,0:T(8,128)(2,1)S(1)}, u32[]{:S(2)}, u32[]{:S(2)}) async-start(bf16[32,40,128]{2,1,0:T(8,128)(2,1)} %pack.1), calls=%async_computation | async-start | bytes 655360 | tf_op jit(solution)/shard_map/all_to_all | solution.py:265
  12.9 1.1 copy-start.4
  14.0 12.1 %copy-start = (bf16[1,1024,224]{1,2,0:T(8,128)(2,1)S(1)}, bf16[1,1024,224]{1,2,0:T(8,128)(2,1)}, u32[]{:S(2)}) copy-start(bf16[1,1024,224]{1,2,0:T(8,128)(2,1)} %param.17) | copy-start | bytes 1376260
  27.3 3.5 %collective-permute-start = (bf16[16,40,256]{2,1,0:T(8,128)(2,1)S(1)}, bf16[16,40,256]{2,1,0:T(8,128)(2,1)S(1)}, u32[]{:S(2)}, u32[]{:S(2)}) collective-permute-start(bf16[16,40,256]{2,1,0:T(8,128)(2,1)S(1)} %get-tuple-element.37), channel_id=1, source_target_pairs={{0,1},{1,0},{2,3},{3,2},{4,5},{5,4},{6,7},{7,6},{8,9},{9,8},{10,11... | collective-permute-start | bytes 983048 | tf_op jit(solution)/shard_map/ppermute | solution.py:284
  71.5 23.1 %copy-start.2 = (bf16[1,224,1024]{2,1,0:T(8,128)(2,1)S(1)}, bf16[1,224,1024]{2,1,0:T(8,128)(2,1)}, u32[]{:S(2)}) copy-start(bf16[1,224,1024]{2,1,0:T(8,128)(2,1)} %param.16) | copy-start | bytes 1376260
  71.6 23.1 %copy-start.1 = (bf16[1,224,1024]{2,1,0:T(8,128)(2,1)S(1)}, bf16[1,224,1024]{2,1,0:T(8,128)(2,1)}, u32[]{:S(2)}) copy-start(bf16[1,224,1024]{2,1,0:T(8,128)(2,1)} %param.15) | copy-start | bytes 1376260
  92.7 3.5 %collective-permute-start.1 = (bf16[16,40,256]{2,1,0:T(8,128)(2,1)S(1)}, bf16[16,40,256]{2,1,0:T(8,128)(2,1)S(1)}, u32[]{:S(2)}, u32[]{:S(2)}) collective-permute-start(bf16[16,40,256]{2,1,0:T(8,128)(2,1)S(1)} %all_to_all.21.refs_0_), channel_id=1, source_target_pairs={{0,1},{1,0},{2,3},{3,2},{4,5},{5,4},{6,7},{7,6},{8,9},{9,8},{10,11... | collective-permute-start | bytes 983048 | tf_op jit(solution)/shard_map/ppermute | solution.py:294
  98.2 16.1 %all-to-all-start.3 = ((bf16[32,24,128]{2,1,0:T(8,128)(2,1)}), bf16[32,24,128]{2,1,0:T(8,128)(2,1)S(1)}, u32[]{:S(2)}, u32[]{:S(2)}) async-start(bf16[32,24,128]{2,1,0:T(8,128)(2,1)} %get-tuple-element.50), calls=%async_computation.3 | async-start | bytes 393216 | tf_op jit(solution)/shard_map/all_to_all | solution.py:313
  103.3 11.1 %copy-start.5 = (s32[32,8]{0,1:T(8,128)S(1)}, s32[32,8]{0,1:T(8,128)}, u32[]{:S(2)}) copy-start(s32[32,8]{0,1:T(8,128)} %param.12) | copy-start | bytes 3076
